TPU v7x, 64 devices: a 2x2x8 block of a 4x4x8 slice. The times are simulated.
64 devices in a mesh: data: 4 (over x, y), ctx: 16 (over z, core).
Axes of the slice: x: 2, y: 2, z: 8, core: 2. Of those that a mesh axis runs over, the one named last changes fastest.
The devices are a block of a 4x4x8 slice.
Arguments:
- queries: bfloat16 [24, 6144, 8, 128], P('data', 'ctx'), parts along dimension 0
- keys_in: bfloat16 [24, 6144, 1, 128], P('data', 'ctx'), parts along dimension 0
- values_in: bfloat16 [24, 6144, 1, 128], P('data', 'ctx'), parts along dimension 0
- grad_out: bfloat16 [24, 6144, 8, 128], P('data', 'ctx'), parts along dimension 0
Outputs:
- output 1: bfloat16 [24, 6144, 8, 128], P('data', 'ctx'), parts along dimension 0
- output 2: bfloat16 [24, 6144, 8, 128], P('data', 'ctx'), parts along dimension 0
- output 3: bfloat16 [24, 6144, 1, 128], P('data', 'ctx'), parts along dimension 0
- output 4: bfloat16 [24, 6144, 1, 128], P('data', 'ctx'), parts along dimension 0
There are 4 independent parts. A program takes and returns all parts, laid end to end along the dimension named above; each array names one.
All inputs are finite; a program needn't handle non-finite values.
Results may differ from a plain program's by a relative error of at most 0.0171987.
Values are sent between devices in bfloat16 or wider.
A program may use at most 768 MiB of HBM per device.

v0:
```python
import jax
import jax.numpy as jnp
from jax import lax
from jax.sharding import PartitionSpec as P

MASK_VALUE = -1e30


def solution(mesh):
    ctx_size = mesh.shape["ctx"]
    block_spec = P("data", "ctx", None, None)
    perm_next = [(dev_id, (dev_id + 1) % ctx_size) for dev_id in range(ctx_size)]

    def local_attention(queries, keys_in, values_in, grad_out):
        batch_size, shard_len, q_heads, head_dim = queries.shape
        kv_heads = keys_in.shape[2]
        group_size = q_heads // kv_heads
        half_len = shard_len // 2
        score_scale = head_dim ** -0.5
        my_index = lax.axis_index("ctx")
        q_five = queries.reshape(batch_size, shard_len, kv_heads, group_size, head_dim)
        g_five = grad_out.reshape(batch_size, shard_len, kv_heads, group_size, head_dim)
        own_mask = jnp.arange(shard_len)[:, None] >= jnp.arange(shard_len)[None, :]

        def scores_of(q_blk, k_blk, mask_tile):
            raw_scores = jnp.einsum("bqhgd,bkhd->bhgqk", q_blk, k_blk, preferred_element_type=jnp.float32) * score_scale
            if mask_tile is None:
                return raw_scores
            return jnp.where(mask_tile, raw_scores, MASK_VALUE)

        def fwd_update(run_state, q_blk, k_blk, v_blk, mask_tile):
            run_max, run_sum, acc_out = run_state
            scores = scores_of(q_blk, k_blk, mask_tile)
            new_max = jnp.maximum(run_max, jnp.max(scores, axis=-1))
            prob_tile = jnp.exp(scores - new_max[..., None])
            decay_factor = jnp.exp(run_max - new_max)
            new_sum = run_sum * decay_factor + jnp.sum(prob_tile, axis=-1)
            pv_part = jnp.einsum("bhgqk,bkhd->bhgqd", prob_tile.astype(jnp.bfloat16), v_blk, preferred_element_type=jnp.float32)
            return new_max, new_sum, acc_out * decay_factor[..., None] + pv_part

        def fwd_past(op_args):
            run_state, k_cur, v_cur = op_args
            return fwd_update(run_state, q_five, k_cur[:, :half_len], v_cur[:, :half_len], None)

        def fwd_future(op_args):
            run_state, k_cur, v_cur = op_args
            low_half = tuple(tensor[:, :, :, :half_len] for tensor in run_state)
            high_half = tuple(tensor[:, :, :, half_len:] for tensor in run_state)
            high_half = fwd_update(high_half, q_five[:, half_len:], k_cur, v_cur, None)
            return tuple(jnp.concatenate([low_part, high_part], axis=3) for low_part, high_part in zip(low_half, high_half))

        def fwd_step(step_idx, loop_carry):
            k_cur, v_cur, run_state = loop_carry
            k_cur = lax.ppermute(k_cur, "ctx", perm_next)
            v_cur = lax.ppermute(v_cur, "ctx", perm_next)
            source_id = (my_index - step_idx) % ctx_size
            run_state = lax.cond(source_id < my_index, fwd_past, fwd_future, (run_state, k_cur, v_cur))
            return k_cur, v_cur, run_state

        stat_shape = (batch_size, kv_heads, group_size, shard_len)
        run_state = (jnp.full(stat_shape, MASK_VALUE, jnp.float32), jnp.zeros(stat_shape, jnp.float32), jnp.zeros(stat_shape + (head_dim,), jnp.float32))
        run_state = fwd_update(run_state, q_five, keys_in, values_in, own_mask)
        loop_out = lax.fori_loop(1, ctx_size, fwd_step, (keys_in, values_in, run_state))
        run_max, run_sum, acc_out = loop_out[2]
        out_heads = (acc_out / run_sum[..., None]).astype(jnp.bfloat16)
        log_sum = run_max + jnp.log(run_sum)
        attn_out = jnp.transpose(out_heads, (0, 3, 1, 2, 4)).reshape(batch_size, shard_len, q_heads, head_dim)
        d_rows = jnp.einsum("bqhgd,bhgqd->bhgq", g_five, out_heads, preferred_element_type=jnp.float32)

        def bwd_block(q_blk, g_blk, lse_blk, drow_blk, k_blk, v_blk, mask_tile):
            prob_tile = jnp.exp(scores_of(q_blk, k_blk, mask_tile) - lse_blk[..., None])
            grad_v = jnp.einsum("bhgqk,bqhgd->bkhd", prob_tile.astype(jnp.bfloat16), g_blk, preferred_element_type=jnp.float32)
            dprob_tile = jnp.einsum("bqhgd,bkhd->bhgqk", g_blk, v_blk, preferred_element_type=jnp.float32)
            dscore_tile = (prob_tile * (dprob_tile - drow_blk[..., None])).astype(jnp.bfloat16)
            grad_q = jnp.einsum("bhgqk,bkhd->bqhgd", dscore_tile, k_blk, preferred_element_type=jnp.float32) * score_scale
            grad_k = jnp.einsum("bhgqk,bqhgd->bkhd", dscore_tile, q_blk, preferred_element_type=jnp.float32) * score_scale
            return grad_q, grad_k, grad_v

        def bwd_past(op_args):
            dq_acc, dk_acc, dv_acc, k_cur, v_cur = op_args
            grad_q, grad_k, grad_v = bwd_block(q_five, g_five, log_sum, d_rows, k_cur[:, :half_len], v_cur[:, :half_len], None)
            dk_acc = jnp.concatenate([dk_acc[:, :half_len] + grad_k, dk_acc[:, half_len:]], axis=1)
            dv_acc = jnp.concatenate([dv_acc[:, :half_len] + grad_v, dv_acc[:, half_len:]], axis=1)
            return dq_acc + grad_q, dk_acc, dv_acc

        def bwd_future(op_args):
            dq_acc, dk_acc, dv_acc, k_cur, v_cur = op_args
            grad_q, grad_k, grad_v = bwd_block(q_five[:, half_len:], g_five[:, half_len:], log_sum[..., half_len:], d_rows[..., half_len:], k_cur, v_cur, None)
            dq_acc = jnp.concatenate([dq_acc[:, :half_len], dq_acc[:, half_len:] + grad_q], axis=1)
            return dq_acc, dk_acc + grad_k, dv_acc + grad_v

        def bwd_step(step_idx, loop_carry):
            dq_acc, dk_acc, dv_acc, k_cur, v_cur = loop_carry
            k_cur = lax.ppermute(k_cur, "ctx", perm_next)
            v_cur = lax.ppermute(v_cur, "ctx", perm_next)
            dk_acc = lax.ppermute(dk_acc, "ctx", perm_next)
            dv_acc = lax.ppermute(dv_acc, "ctx", perm_next)
            source_id = (my_index - step_idx) % ctx_size
            dq_acc, dk_acc, dv_acc = lax.cond(source_id < my_index, bwd_past, bwd_future, (dq_acc, dk_acc, dv_acc, k_cur, v_cur))
            return dq_acc, dk_acc, dv_acc, k_cur, v_cur

        first_grads = bwd_block(q_five, g_five, log_sum, d_rows, keys_in, values_in, own_mask)
        loop_out = lax.fori_loop(1, ctx_size, bwd_step, first_grads + (keys_in, values_in))
        grad_k = lax.ppermute(loop_out[1], "ctx", perm_next)
        grad_v = lax.ppermute(loop_out[2], "ctx", perm_next)
        grad_q = loop_out[0].reshape(batch_size, shard_len, q_heads, head_dim).astype(jnp.bfloat16)
        return attn_out, grad_q, grad_k.astype(jnp.bfloat16), grad_v.astype(jnp.bfloat16)

    return jax.shard_map(local_attention, mesh=mesh, in_specs=(block_spec,) * 4, out_specs=(block_spec,) * 4, check_vma=False)
```

profile of v0, /device:TPU:21, one launch (start us, length us, event | category | flops | bytes accessed | tf_op | source)
XLA Modules:
  0.0 2290.0 jit_solution(8801558050124612690)
XLA Ops:
  60.8 775.0 %while.46 = (s32[]{:T(128)}, bf16[6,384,1,128]{3,1,0,2:T(8,128)(2,1)}, bf16[6,384,1,128]{3,1,0,2:T(8,128)(2,1)}, f32[6,1,8,384]{3,2,0,1:T(8,128)S(1)}, f32[6,1,8...) while((s32[]{:T(128)}, ...), condition=%wide.region_9.10_spmd, body=%wide.region_2.9_spmd.sunk | while | flops 1845033984 | bytes 140968496 | solution.py:63
  910.9 1336.2 %while.47 = (s32[]{:T(128)}, f32[6,384,1,8,128]{4,1,3,0,2:T(8,128)}, f32[6,384,1,128]{3,1,0,2:T(8,128)}, f32[6,384,1,128]{3,1,0,2:T(8,128)}, bf16[6,384,1,128]{3...) while((s32[]{:T(128)}, ...), condition=%wide.region_13.14_spmd, body=%wide.region_10.13_spmd.sunk | while | flops 4563910656 | bytes 249754512 | solution.py:103
  1033.0 46.9 %conditional.5 = (f32[6,384,1,8,128]{4,1,3,0,2:T(8,128)}, f32[6,384,1,128]{3,1,0,2:T(8,128)}, f32[6,384,1,128]{3,1,0,2:T(8,128)}) conditional(s32[]{:T(128)} %convert_element_type.123, (f32[6,384,1,8,128]{4,1,3,0,2:T(8,128)}, bf16[6,384,1,128]{3,1,0,2:T(8,128)(2,1)S(1)}, bf16[6,384,1,8,128]{4,1,3,0,2:T(8,128)(2,1)}, f32[6,1,8,384]{3,2,0,1:T(8,128)}, ...), branch_computations={%region_11.11_spmd, %region_12.12_spmd} | conditional | flops 4563910656 | bytes 233238848 | solution.py:99
  1121.8 46.9 %conditional.5 = (f32[6,384,1,8,128]{4,1,3,0,2:T(8,128)}, f32[6,384,1,128]{3,1,0,2:T(8,128)}, f32[6,384,1,128]{3,1,0,2:T(8,128)}) conditional(s32[]{:T(128)} %convert_element_type.123, (f32[6,384,1,8,128]{4,1,3,0,2:T(8,128)}, bf16[6,384,1,128]{3,1,0,2:T(8,128)(2,1)S(1)}, bf16[6,384,1,8,128]{4,1,3,0,2:T(8,128)(2,1)}, f32[6,1,8,384]{3,2,0,1:T(8,128)}, ...), branch_computations={%region_11.11_spmd, %region_12.12_spmd} | conditional | flops 4563910656 | bytes 233238848 | solution.py:99
  1168.9 41.1 %collective-permute-done.2 = bf16[6,384,1,128]{3,1,0,2:T(8,128)(2,1)S(1)} collective-permute-done((bf16[6,384,1,128]{3,1,0,2:T(8,128)(2,1)}, bf16[6,384,1,128]{3,1,0,2:T(8,128)(2,1)S(1)}, u32[]{:S(2)}, u32[]{:S(2)}) %collective-permute-start.2) | collective-permute-done | bytes 589856 | tf_op jit(solution)/shard_map/while/body/eval_jaxpr/ppermute | solution.py:94
  1211.7 46.9 %conditional.5 = (f32[6,384,1,8,128]{4,1,3,0,2:T(8,128)}, f32[6,384,1,128]{3,1,0,2:T(8,128)}, f32[6,384,1,128]{3,1,0,2:T(8,128)}) conditional(s32[]{:T(128)} %convert_element_type.123, (f32[6,384,1,8,128]{4,1,3,0,2:T(8,128)}, bf16[6,384,1,128]{3,1,0,2:T(8,128)(2,1)S(1)}, bf16[6,384,1,8,128]{4,1,3,0,2:T(8,128)(2,1)}, f32[6,1,8,384]{3,2,0,1:T(8,128)}, ...), branch_computations={%region_11.11_spmd, %region_12.12_spmd} | conditional | flops 4563910656 | bytes 233238848 | solution.py:99
  1258.7 41.1 %collective-permute-done.2 = bf16[6,384,1,128]{3,1,0,2:T(8,128)(2,1)S(1)} collective-permute-done((bf16[6,384,1,128]{3,1,0,2:T(8,128)(2,1)}, bf16[6,384,1,128]{3,1,0,2:T(8,128)(2,1)S(1)}, u32[]{:S(2)}, u32[]{:S(2)}) %collective-permute-start.2) | collective-permute-done | bytes 589856 | tf_op jit(solution)/shard_map/while/body/eval_jaxpr/ppermute | solution.py:94
  1301.5 46.9 %conditional.5 = (f32[6,384,1,8,128]{4,1,3,0,2:T(8,128)}, f32[6,384,1,128]{3,1,0,2:T(8,128)}, f32[6,384,1,128]{3,1,0,2:T(8,128)}) conditional(s32[]{:T(128)} %convert_element_type.123, (f32[6,384,1,8,128]{4,1,3,0,2:T(8,128)}, bf16[6,384,1,128]{3,1,0,2:T(8,128)(2,1)S(1)}, bf16[6,384,1,8,128]{4,1,3,0,2:T(8,128)(2,1)}, f32[6,1,8,384]{3,2,0,1:T(8,128)}, ...), branch_computations={%region_11.11_spmd, %region_12.12_spmd} | conditional | flops 4563910656 | bytes 233238848 | solution.py:99
  1348.6 41.1 %collective-permute-done.2 = bf16[6,384,1,128]{3,1,0,2:T(8,128)(2,1)S(1)} collective-permute-done((bf16[6,384,1,128]{3,1,0,2:T(8,128)(2,1)}, bf16[6,384,1,128]{3,1,0,2:T(8,128)(2,1)S(1)}, u32[]{:S(2)}, u32[]{:S(2)}) %collective-permute-start.2) | collective-permute-done | bytes 589856 | tf_op jit(solution)/shard_map/while/body/eval_jaxpr/ppermute | solution.py:94
  1391.4 46.9 %conditional.5 = (f32[6,384,1,8,128]{4,1,3,0,2:T(8,128)}, f32[6,384,1,128]{3,1,0,2:T(8,128)}, f32[6,384,1,128]{3,1,0,2:T(8,128)}) conditional(s32[]{:T(128)} %convert_element_type.123, (f32[6,384,1,8,128]{4,1,3,0,2:T(8,128)}, bf16[6,384,1,128]{3,1,0,2:T(8,128)(2,1)S(1)}, bf16[6,384,1,8,128]{4,1,3,0,2:T(8,128)(2,1)}, f32[6,1,8,384]{3,2,0,1:T(8,128)}, ...), branch_computations={%region_11.11_spmd, %region_12.12_spmd} | conditional | flops 4563910656 | bytes 233238848 | solution.py:99
  1438.4 41.1 %collective-permute-done.2 = bf16[6,384,1,128]{3,1,0,2:T(8,128)(2,1)S(1)} collective-permute-done((bf16[6,384,1,128]{3,1,0,2:T(8,128)(2,1)}, bf16[6,384,1,128]{3,1,0,2:T(8,128)(2,1)S(1)}, u32[]{:S(2)}, u32[]{:S(2)}) %collective-permute-start.2) | collective-permute-done | bytes 589856 | tf_op jit(solution)/shard_map/while/body/eval_jaxpr/ppermute | solution.py:94
  1481.2 46.9 %conditional.5 = (f32[6,384,1,8,128]{4,1,3,0,2:T(8,128)}, f32[6,384,1,128]{3,1,0,2:T(8,128)}, f32[6,384,1,128]{3,1,0,2:T(8,128)}) conditional(s32[]{:T(128)} %convert_element_type.123, (f32[6,384,1,8,128]{4,1,3,0,2:T(8,128)}, bf16[6,384,1,128]{3,1,0,2:T(8,128)(2,1)S(1)}, bf16[6,384,1,8,128]{4,1,3,0,2:T(8,128)(2,1)}, f32[6,1,8,384]{3,2,0,1:T(8,128)}, ...), branch_computations={%region_11.11_spmd, %region_12.12_spmd} | conditional | flops 4563910656 | bytes 233238848 | solution.py:99
  1571.1 46.9 %conditional.5 = (f32[6,384,1,8,128]{4,1,3,0,2:T(8,128)}, f32[6,384,1,128]{3,1,0,2:T(8,128)}, f32[6,384,1,128]{3,1,0,2:T(8,128)}) conditional(s32[]{:T(128)} %convert_element_type.123, (f32[6,384,1,8,128]{4,1,3,0,2:T(8,128)}, bf16[6,384,1,128]{3,1,0,2:T(8,128)(2,1)S(1)}, bf16[6,384,1,8,128]{4,1,3,0,2:T(8,128)(2,1)}, f32[6,1,8,384]{3,2,0,1:T(8,128)}, ...), branch_computations={%region_11.11_spmd, %region_12.12_spmd} | conditional | flops 4563910656 | bytes 233238848 | solution.py:99
  1618.1 41.1 %collective-permute-done.2 = bf16[6,384,1,128]{3,1,0,2:T(8,128)(2,1)S(1)} collective-permute-done((bf16[6,384,1,128]{3,1,0,2:T(8,128)(2,1)}, bf16[6,384,1,128]{3,1,0,2:T(8,128)(2,1)S(1)}, u32[]{:S(2)}, u32[]{:S(2)}) %collective-permute-start.2) | collective-permute-done | bytes 589856 | tf_op jit(solution)/shard_map/while/body/eval_jaxpr/ppermute | solution.py:94
  1660.9 46.9 %conditional.5 = (f32[6,384,1,8,128]{4,1,3,0,2:T(8,128)}, f32[6,384,1,128]{3,1,0,2:T(8,128)}, f32[6,384,1,128]{3,1,0,2:T(8,128)}) conditional(s32[]{:T(128)} %convert_element_type.123, (f32[6,384,1,8,128]{4,1,3,0,2:T(8,128)}, bf16[6,384,1,128]{3,1,0,2:T(8,128)(2,1)S(1)}, bf16[6,384,1,8,128]{4,1,3,0,2:T(8,128)(2,1)}, f32[6,1,8,384]{3,2,0,1:T(8,128)}, ...), branch_computations={%region_11.11_spmd, %region_12.12_spmd} | conditional | flops 4563910656 | bytes 233238848 | solution.py:99
  1750.8 46.9 %conditional.5 = (f32[6,384,1,8,128]{4,1,3,0,2:T(8,128)}, f32[6,384,1,128]{3,1,0,2:T(8,128)}, f32[6,384,1,128]{3,1,0,2:T(8,128)}) conditional(s32[]{:T(128)} %convert_element_type.123, (f32[6,384,1,8,128]{4,1,3,0,2:T(8,128)}, bf16[6,384,1,128]{3,1,0,2:T(8,128)(2,1)S(1)}, bf16[6,384,1,8,128]{4,1,3,0,2:T(8,128)(2,1)}, f32[6,1,8,384]{3,2,0,1:T(8,128)}, ...), branch_computations={%region_11.11_spmd, %region_12.12_spmd} | conditional | flops 4563910656 | bytes 233238848 | solution.py:99
  1797.8 41.1 %collective-permute-done.2 = bf16[6,384,1,128]{3,1,0,2:T(8,128)(2,1)S(1)} collective-permute-done((bf16[6,384,1,128]{3,1,0,2:T(8,128)(2,1)}, bf16[6,384,1,128]{3,1,0,2:T(8,128)(2,1)S(1)}, u32[]{:S(2)}, u32[]{:S(2)}) %collective-permute-start.2) | collective-permute-done | bytes 589856 | tf_op jit(solution)/shard_map/while/body/eval_jaxpr/ppermute | solution.py:94
  1840.6 46.9 %conditional.5 = (f32[6,384,1,8,128]{4,1,3,0,2:T(8,128)}, f32[6,384,1,128]{3,1,0,2:T(8,128)}, f32[6,384,1,128]{3,1,0,2:T(8,128)}) conditional(s32[]{:T(128)} %convert_element_type.123, (f32[6,384,1,8,128]{4,1,3,0,2:T(8,128)}, bf16[6,384,1,128]{3,1,0,2:T(8,128)(2,1)S(1)}, bf16[6,384,1,8,128]{4,1,3,0,2:T(8,128)(2,1)}, f32[6,1,8,384]{3,2,0,1:T(8,128)}, ...), branch_computations={%region_11.11_spmd, %region_12.12_spmd} | conditional | flops 4563910656 | bytes 233238848 | solution.py:99
  1930.5 46.9 %conditional.5 = (f32[6,384,1,8,128]{4,1,3,0,2:T(8,128)}, f32[6,384,1,128]{3,1,0,2:T(8,128)}, f32[6,384,1,128]{3,1,0,2:T(8,128)}) conditional(s32[]{:T(128)} %convert_element_type.123, (f32[6,384,1,8,128]{4,1,3,0,2:T(8,128)}, bf16[6,384,1,128]{3,1,0,2:T(8,128)(2,1)S(1)}, bf16[6,384,1,8,128]{4,1,3,0,2:T(8,128)(2,1)}, f32[6,1,8,384]{3,2,0,1:T(8,128)}, ...), branch_computations={%region_11.11_spmd, %region_12.12_spmd} | conditional | flops 4563910656 | bytes 233238848 | solution.py:99
  1977.5 41.1 %collective-permute-done.2 = bf16[6,384,1,128]{3,1,0,2:T(8,128)(2,1)S(1)} collective-permute-done((bf16[6,384,1,128]{3,1,0,2:T(8,128)(2,1)}, bf16[6,384,1,128]{3,1,0,2:T(8,128)(2,1)S(1)}, u32[]{:S(2)}, u32[]{:S(2)}) %collective-permute-start.2) | collective-permute-done | bytes 589856 | tf_op jit(solution)/shard_map/while/body/eval_jaxpr/ppermute | solution.py:94
  2020.3 46.9 %conditional.5 = (f32[6,384,1,8,128]{4,1,3,0,2:T(8,128)}, f32[6,384,1,128]{3,1,0,2:T(8,128)}, f32[6,384,1,128]{3,1,0,2:T(8,128)}) conditional(s32[]{:T(128)} %convert_element_type.123, (f32[6,384,1,8,128]{4,1,3,0,2:T(8,128)}, bf16[6,384,1,128]{3,1,0,2:T(8,128)(2,1)S(1)}, bf16[6,384,1,8,128]{4,1,3,0,2:T(8,128)(2,1)}, f32[6,1,8,384]{3,2,0,1:T(8,128)}, ...), branch_computations={%region_11.11_spmd, %region_12.12_spmd} | conditional | flops 4563910656 | bytes 233238848 | solution.py:99
  2067.4 41.1 %collective-permute-done.2 = bf16[6,384,1,128]{3,1,0,2:T(8,128)(2,1)S(1)} collective-permute-done((bf16[6,384,1,128]{3,1,0,2:T(8,128)(2,1)}, bf16[6,384,1,128]{3,1,0,2:T(8,128)(2,1)S(1)}, u32[]{:S(2)}, u32[]{:S(2)}) %collective-permute-start.2) | collective-permute-done | bytes 589856 | tf_op jit(solution)/shard_map/while/body/eval_jaxpr/ppermute | solution.py:94
  2110.2 46.9 %conditional.5 = (f32[6,384,1,8,128]{4,1,3,0,2:T(8,128)}, f32[6,384,1,128]{3,1,0,2:T(8,128)}, f32[6,384,1,128]{3,1,0,2:T(8,128)}) conditional(s32[]{:T(128)} %convert_element_type.123, (f32[6,384,1,8,128]{4,1,3,0,2:T(8,128)}, bf16[6,384,1,128]{3,1,0,2:T(8,128)(2,1)S(1)}, bf16[6,384,1,8,128]{4,1,3,0,2:T(8,128)(2,1)}, f32[6,1,8,384]{3,2,0,1:T(8,128)}, ...), branch_computations={%region_11.11_spmd, %region_12.12_spmd} | conditional | flops 4563910656 | bytes 233238848 | solution.py:99
  2200.0 46.9 %conditional.5 = (f32[6,384,1,8,128]{4,1,3,0,2:T(8,128)}, f32[6,384,1,128]{3,1,0,2:T(8,128)}, f32[6,384,1,128]{3,1,0,2:T(8,128)}) conditional(s32[]{:T(128)} %convert_element_type.123, (f32[6,384,1,8,128]{4,1,3,0,2:T(8,128)}, bf16[6,384,1,128]{3,1,0,2:T(8,128)(2,1)S(1)}, bf16[6,384,1,8,128]{4,1,3,0,2:T(8,128)(2,1)}, f32[6,1,8,384]{3,2,0,1:T(8,128)}, ...), branch_computations={%region_11.11_spmd, %region_12.12_spmd} | conditional | flops 4563910656 | bytes 233238848 | solution.py:99
  (978 shorter events, 2412.9 us)
Async XLA Ops:
  1168.7 43.0 %collective-permute-start.4 = (f32[6,384,1,128]{3,1,0,2:T(8,128)}, f32[6,384,1,128]{3,1,0,2:T(8,128)S(1)}, u32[]{:S(2)}, u32[]{:S(2)}) collective-permute-start(f32[6,384,1,128]{3,1,0,2:T(8,128)} %get-tuple-element.880), channel_id=1, source_target_pairs={{0,1},{1,2},{2,3},{3,4},{4,5},{5,6},{6,7},{7,8},{8,9},{9,10},{10,1... | collective-permute-start | bytes 3538952 | tf_op jit(solution)/shard_map/while/body/eval_jaxpr/ppermute | solution.py:96
  1168.7 43.0 %collective-permute-start.5 = (f32[6,384,1,128]{3,1,0,2:T(8,128)}, f32[6,384,1,128]{3,1,0,2:T(8,128)S(1)}, u32[]{:S(2)}, u32[]{:S(2)}) collective-permute-start(f32[6,384,1,128]{3,1,0,2:T(8,128)} %get-tuple-element.881), channel_id=1, source_target_pairs={{0,1},{1,2},{2,3},{3,4},{4,5},{5,6},{6,7},{7,8},{8,9},{9,10},{10,1... | collective-permute-start | bytes 3538952 | tf_op jit(solution)/shard_map/while/body/eval_jaxpr/ppermute | solution.py:97
  1258.5 43.0 %collective-permute-start.4 = (f32[6,384,1,128]{3,1,0,2:T(8,128)}, f32[6,384,1,128]{3,1,0,2:T(8,128)S(1)}, u32[]{:S(2)}, u32[]{:S(2)}) collective-permute-start(f32[6,384,1,128]{3,1,0,2:T(8,128)} %get-tuple-element.880), channel_id=1, source_target_pairs={{0,1},{1,2},{2,3},{3,4},{4,5},{5,6},{6,7},{7,8},{8,9},{9,10},{10,1... | collective-permute-start | bytes 3538952 | tf_op jit(solution)/shard_map/while/body/eval_jaxpr/ppermute | solution.py:96
  1258.5 43.0 %collective-permute-start.5 = (f32[6,384,1,128]{3,1,0,2:T(8,128)}, f32[6,384,1,128]{3,1,0,2:T(8,128)S(1)}, u32[]{:S(2)}, u32[]{:S(2)}) collective-permute-start(f32[6,384,1,128]{3,1,0,2:T(8,128)} %get-tuple-element.881), channel_id=1, source_target_pairs={{0,1},{1,2},{2,3},{3,4},{4,5},{5,6},{6,7},{7,8},{8,9},{9,10},{10,1... | collective-permute-start | bytes 3538952 | tf_op jit(solution)/shard_map/while/body/eval_jaxpr/ppermute | solution.py:97
  1348.4 43.0 %collective-permute-start.4 = (f32[6,384,1,128]{3,1,0,2:T(8,128)}, f32[6,384,1,128]{3,1,0,2:T(8,128)S(1)}, u32[]{:S(2)}, u32[]{:S(2)}) collective-permute-start(f32[6,384,1,128]{3,1,0,2:T(8,128)} %get-tuple-element.880), channel_id=1, source_target_pairs={{0,1},{1,2},{2,3},{3,4},{4,5},{5,6},{6,7},{7,8},{8,9},{9,10},{10,1... | collective-permute-start | bytes 3538952 | tf_op jit(solution)/shard_map/while/body/eval_jaxpr/ppermute | solution.py:96
  1348.4 43.0 %collective-permute-start.5 = (f32[6,384,1,128]{3,1,0,2:T(8,128)}, f32[6,384,1,128]{3,1,0,2:T(8,128)S(1)}, u32[]{:S(2)}, u32[]{:S(2)}) collective-permute-start(f32[6,384,1,128]{3,1,0,2:T(8,128)} %get-tuple-element.881), channel_id=1, source_target_pairs={{0,1},{1,2},{2,3},{3,4},{4,5},{5,6},{6,7},{7,8},{8,9},{9,10},{10,1... | collective-permute-start | bytes 3538952 | tf_op jit(solution)/shard_map/while/body/eval_jaxpr/ppermute | solution.py:97
  1438.3 43.0 %collective-permute-start.4 = (f32[6,384,1,128]{3,1,0,2:T(8,128)}, f32[6,384,1,128]{3,1,0,2:T(8,128)S(1)}, u32[]{:S(2)}, u32[]{:S(2)}) collective-permute-start(f32[6,384,1,128]{3,1,0,2:T(8,128)} %get-tuple-element.880), channel_id=1, source_target_pairs={{0,1},{1,2},{2,3},{3,4},{4,5},{5,6},{6,7},{7,8},{8,9},{9,10},{10,1... | collective-permute-start | bytes 3538952 | tf_op jit(solution)/shard_map/while/body/eval_jaxpr/ppermute | solution.py:96
  1438.3 43.0 %collective-permute-start.5 = (f32[6,384,1,128]{3,1,0,2:T(8,128)}, f32[6,384,1,128]{3,1,0,2:T(8,128)S(1)}, u32[]{:S(2)}, u32[]{:S(2)}) collective-permute-start(f32[6,384,1,128]{3,1,0,2:T(8,128)} %get-tuple-element.881), channel_id=1, source_target_pairs={{0,1},{1,2},{2,3},{3,4},{4,5},{5,6},{6,7},{7,8},{8,9},{9,10},{10,1... | collective-permute-start | bytes 3538952 | tf_op jit(solution)/shard_map/while/body/eval_jaxpr/ppermute | solution.py:97
  1528.1 43.0 %collective-permute-start.4 = (f32[6,384,1,128]{3,1,0,2:T(8,128)}, f32[6,384,1,128]{3,1,0,2:T(8,128)S(1)}, u32[]{:S(2)}, u32[]{:S(2)}) collective-permute-start(f32[6,384,1,128]{3,1,0,2:T(8,128)} %get-tuple-element.880), channel_id=1, source_target_pairs={{0,1},{1,2},{2,3},{3,4},{4,5},{5,6},{6,7},{7,8},{8,9},{9,10},{10,1... | collective-permute-start | bytes 3538952 | tf_op jit(solution)/shard_map/while/body/eval_jaxpr/ppermute | solution.py:96
  1528.1 43.0 %collective-permute-start.5 = (f32[6,384,1,128]{3,1,0,2:T(8,128)}, f32[6,384,1,128]{3,1,0,2:T(8,128)S(1)}, u32[]{:S(2)}, u32[]{:S(2)}) collective-permute-start(f32[6,384,1,128]{3,1,0,2:T(8,128)} %get-tuple-element.881), channel_id=1, source_target_pairs={{0,1},{1,2},{2,3},{3,4},{4,5},{5,6},{6,7},{7,8},{8,9},{9,10},{10,1... | collective-permute-start | bytes 3538952 | tf_op jit(solution)/shard_map/while/body/eval_jaxpr/ppermute | solution.py:97
  1618.0 43.0 %collective-permute-start.4 = (f32[6,384,1,128]{3,1,0,2:T(8,128)}, f32[6,384,1,128]{3,1,0,2:T(8,128)S(1)}, u32[]{:S(2)}, u32[]{:S(2)}) collective-permute-start(f32[6,384,1,128]{3,1,0,2:T(8,128)} %get-tuple-element.880), channel_id=1, source_target_pairs={{0,1},{1,2},{2,3},{3,4},{4,5},{5,6},{6,7},{7,8},{8,9},{9,10},{10,1... | collective-permute-start | bytes 3538952 | tf_op jit(solution)/shard_map/while/body/eval_jaxpr/ppermute | solution.py:96
  1618.0 43.0 %collective-permute-start.5 = (f32[6,384,1,128]{3,1,0,2:T(8,128)}, f32[6,384,1,128]{3,1,0,2:T(8,128)S(1)}, u32[]{:S(2)}, u32[]{:S(2)}) collective-permute-start(f32[6,384,1,128]{3,1,0,2:T(8,128)} %get-tuple-element.881), channel_id=1, source_target_pairs={{0,1},{1,2},{2,3},{3,4},{4,5},{5,6},{6,7},{7,8},{8,9},{9,10},{10,1... | collective-permute-start | bytes 3538952 | tf_op jit(solution)/shard_map/while/body/eval_jaxpr/ppermute | solution.py:97
  1707.8 43.0 %collective-permute-start.4 = (f32[6,384,1,128]{3,1,0,2:T(8,128)}, f32[6,384,1,128]{3,1,0,2:T(8,128)S(1)}, u32[]{:S(2)}, u32[]{:S(2)}) collective-permute-start(f32[6,384,1,128]{3,1,0,2:T(8,128)} %get-tuple-element.880), channel_id=1, source_target_pairs={{0,1},{1,2},{2,3},{3,4},{4,5},{5,6},{6,7},{7,8},{8,9},{9,10},{10,1... | collective-permute-start | bytes 3538952 | tf_op jit(solution)/shard_map/while/body/eval_jaxpr/ppermute | solution.py:96
  1707.8 43.0 %collective-permute-start.5 = (f32[6,384,1,128]{3,1,0,2:T(8,128)}, f32[6,384,1,128]{3,1,0,2:T(8,128)S(1)}, u32[]{:S(2)}, u32[]{:S(2)}) collective-permute-start(f32[6,384,1,128]{3,1,0,2:T(8,128)} %get-tuple-element.881), channel_id=1, source_target_pairs={{0,1},{1,2},{2,3},{3,4},{4,5},{5,6},{6,7},{7,8},{8,9},{9,10},{10,1... | collective-permute-start | bytes 3538952 | tf_op jit(solution)/shard_map/while/body/eval_jaxpr/ppermute | solution.py:97
  1797.7 43.0 %collective-permute-start.4 = (f32[6,384,1,128]{3,1,0,2:T(8,128)}, f32[6,384,1,128]{3,1,0,2:T(8,128)S(1)}, u32[]{:S(2)}, u32[]{:S(2)}) collective-permute-start(f32[6,384,1,128]{3,1,0,2:T(8,128)} %get-tuple-element.880), channel_id=1, source_target_pairs={{0,1},{1,2},{2,3},{3,4},{4,5},{5,6},{6,7},{7,8},{8,9},{9,10},{10,1... | collective-permute-start | bytes 3538952 | tf_op jit(solution)/shard_map/while/body/eval_jaxpr/ppermute | solution.py:96
  1797.7 43.0 %collective-permute-start.5 = (f32[6,384,1,128]{3,1,0,2:T(8,128)}, f32[6,384,1,128]{3,1,0,2:T(8,128)S(1)}, u32[]{:S(2)}, u32[]{:S(2)}) collective-permute-start(f32[6,384,1,128]{3,1,0,2:T(8,128)} %get-tuple-element.881), channel_id=1, source_target_pairs={{0,1},{1,2},{2,3},{3,4},{4,5},{5,6},{6,7},{7,8},{8,9},{9,10},{10,1... | collective-permute-start | bytes 3538952 | tf_op jit(solution)/shard_map/while/body/eval_jaxpr/ppermute | solution.py:97
  1887.5 43.0 %collective-permute-start.4 = (f32[6,384,1,128]{3,1,0,2:T(8,128)}, f32[6,384,1,128]{3,1,0,2:T(8,128)S(1)}, u32[]{:S(2)}, u32[]{:S(2)}) collective-permute-start(f32[6,384,1,128]{3,1,0,2:T(8,128)} %get-tuple-element.880), channel_id=1, source_target_pairs={{0,1},{1,2},{2,3},{3,4},{4,5},{5,6},{6,7},{7,8},{8,9},{9,10},{10,1... | collective-permute-start | bytes 3538952 | tf_op jit(solution)/shard_map/while/body/eval_jaxpr/ppermute | solution.py:96
  1887.5 43.0 %collective-permute-start.5 = (f32[6,384,1,128]{3,1,0,2:T(8,128)}, f32[6,384,1,128]{3,1,0,2:T(8,128)S(1)}, u32[]{:S(2)}, u32[]{:S(2)}) collective-permute-start(f32[6,384,1,128]{3,1,0,2:T(8,128)} %get-tuple-element.881), channel_id=1, source_target_pairs={{0,1},{1,2},{2,3},{3,4},{4,5},{5,6},{6,7},{7,8},{8,9},{9,10},{10,1... | collective-permute-start | bytes 3538952 | tf_op jit(solution)/shard_map/while/body/eval_jaxpr/ppermute | solution.py:97
  1977.4 43.0 %collective-permute-start.4 = (f32[6,384,1,128]{3,1,0,2:T(8,128)}, f32[6,384,1,128]{3,1,0,2:T(8,128)S(1)}, u32[]{:S(2)}, u32[]{:S(2)}) collective-permute-start(f32[6,384,1,128]{3,1,0,2:T(8,128)} %get-tuple-element.880), channel_id=1, source_target_pairs={{0,1},{1,2},{2,3},{3,4},{4,5},{5,6},{6,7},{7,8},{8,9},{9,10},{10,1... | collective-permute-start | bytes 3538952 | tf_op jit(solution)/shard_map/while/body/eval_jaxpr/ppermute | solution.py:96
  1977.4 43.0 %collective-permute-start.5 = (f32[6,384,1,128]{3,1,0,2:T(8,128)}, f32[6,384,1,128]{3,1,0,2:T(8,128)S(1)}, u32[]{:S(2)}, u32[]{:S(2)}) collective-permute-start(f32[6,384,1,128]{3,1,0,2:T(8,128)} %get-tuple-element.881), channel_id=1, source_target_pairs={{0,1},{1,2},{2,3},{3,4},{4,5},{5,6},{6,7},{7,8},{8,9},{9,10},{10,1... | collective-permute-start | bytes 3538952 | tf_op jit(solution)/shard_map/while/body/eval_jaxpr/ppermute | solution.py:97
  2067.2 43.0 %collective-permute-start.4 = (f32[6,384,1,128]{3,1,0,2:T(8,128)}, f32[6,384,1,128]{3,1,0,2:T(8,128)S(1)}, u32[]{:S(2)}, u32[]{:S(2)}) collective-permute-start(f32[6,384,1,128]{3,1,0,2:T(8,128)} %get-tuple-element.880), channel_id=1, source_target_pairs={{0,1},{1,2},{2,3},{3,4},{4,5},{5,6},{6,7},{7,8},{8,9},{9,10},{10,1... | collective-permute-start | bytes 3538952 | tf_op jit(solution)/shard_map/while/body/eval_jaxpr/ppermute | solution.py:96
  2067.2 43.0 %collective-permute-start.5 = (f32[6,384,1,128]{3,1,0,2:T(8,128)}, f32[6,384,1,128]{3,1,0,2:T(8,128)S(1)}, u32[]{:S(2)}, u32[]{:S(2)}) collective-permute-start(f32[6,384,1,128]{3,1,0,2:T(8,128)} %get-tuple-element.881), channel_id=1, source_target_pairs={{0,1},{1,2},{2,3},{3,4},{4,5},{5,6},{6,7},{7,8},{8,9},{9,10},{10,1... | collective-permute-start | bytes 3538952 | tf_op jit(solution)/shard_map/while/body/eval_jaxpr/ppermute | solution.py:97
  2157.1 43.0 %collective-permute-start.4 = (f32[6,384,1,128]{3,1,0,2:T(8,128)}, f32[6,384,1,128]{3,1,0,2:T(8,128)S(1)}, u32[]{:S(2)}, u32[]{:S(2)}) collective-permute-start(f32[6,384,1,128]{3,1,0,2:T(8,128)} %get-tuple-element.880), channel_id=1, source_target_pairs={{0,1},{1,2},{2,3},{3,4},{4,5},{5,6},{6,7},{7,8},{8,9},{9,10},{10,1... | collective-permute-start | bytes 3538952 | tf_op jit(solution)/shard_map/while/body/eval_jaxpr/ppermute | solution.py:96
  2157.1 43.0 %collective-permute-start.5 = (f32[6,384,1,128]{3,1,0,2:T(8,128)}, f32[6,384,1,128]{3,1,0,2:T(8,128)S(1)}, u32[]{:S(2)}, u32[]{:S(2)}) collective-permute-start(f32[6,384,1,128]{3,1,0,2:T(8,128)} %get-tuple-element.881), channel_id=1, source_target_pairs={{0,1},{1,2},{2,3},{3,4},{4,5},{5,6},{6,7},{7,8},{8,9},{9,10},{10,1... | collective-permute-start | bytes 3538952 | tf_op jit(solution)/shard_map/while/body/eval_jaxpr/ppermute | solution.py:97
  (270 other events, 4667.4 us)
where the time goes:
time: 2310 us; the launch traced here: 2290 us
  waiting for transfers between devices  782 us (34%)
  matrix products  770 us (33%)
  other arithmetic  334 us (14%)
  local copies, waits for them, and re-layouts  252 us (11%)
  starting transfers between devices  146 us (6%)
    ppermute x15, waiting for transfers between devices, bwd_step(): k_cur = lax.ppermute(k_cur, 'ctx', perm_next)  592 us
    dot_general x31, matrix products, scores_of(): jnp.einsum('bqhgd,bkhd->bhgqk', q_blk, k_blk, preferred_element_type=jnp....  160 us
    dot_general x16, matrix products, bwd_block(): jnp.einsum('bhgqk,bqhgd->bkhd', prob_tile.astype(jnp.bfloat16), g_blk, pr...  158 us
    dot_general x16, matrix products, bwd_block(): jnp.einsum('bqhgd,bkhd->bhgqk', g_blk, v_blk, preferred_element_type=jnp....  141 us
    concatenate x28, other arithmetic, fwd_future(): jnp.concatenate([low_part, high_part], axis=3)  129 us
    dot_general x16, matrix products, fwd_update(): jnp.einsum('bhgqk,bkhd->bhgqd', prob_tile.astype(jnp.bfloat16), v_blk, pr...  123 us
    dot_general x16, matrix products, bwd_block(): jnp.einsum('bhgqk,bqhgd->bkhd', dscore_tile, q_blk, preferred_element_typ...  108 us
    ppermute x15, waiting for transfers between devices, fwd_step(): k_cur = lax.ppermute(k_cur, 'ctx', perm_next)  98.7 us
  transfers between devices with their start and end apart: 92, of which 48 were waited for; matrix products, arithmetic and copies ran while one was open for 2% of the time, Pallas kernels for 0%

commit v1 on v0

v1 whole, which is shorter than its diff:
```python
import functools
import math

import jax
import jax.numpy as jnp
from jax import lax
from jax.experimental import pallas as pl
from jax.experimental.pallas import tpu as pltpu
from jax.sharding import PartitionSpec as P

MASK_VALUE = -1e30
BIG = 1024
SUB = 256
POS = 64
VMEM_BYTES = 60 * 2**20


def _dot(lhs, rhs):
    return lax.dot_general(lhs, rhs, (((1,), (0,)), ((), ())), preferred_element_type=jnp.float32)


def _attention_sequence(my_index, ctx_size, heads, q_ref, g_ref, k_ref, v_ref, o_ref, dq_ref, dk_ref, dv_ref, work):
    kt_ref, vt_ref, strip, qt_ref, gt_ref, ot_ref, dqt_ref, m_ref, l_ref = work
    seq_len, head_dim = k_ref.shape
    rows = q_ref.shape[0]
    half_len = rows // heads // 2
    tile = POS * heads
    scale = head_dim**-0.5
    log2_scale = scale * math.log2(math.e)
    last_piece = 2 * ctx_size - 1

    def prepare(step, carry):
        span = pl.ds(pl.multiple_of(step * BIG, BIG), BIG)
        kt_ref[:, span] = k_ref[span, :].T
        vt_ref[:, span] = v_ref[span, :].T
        dk_ref[span, :] = jnp.zeros((BIG, head_dim), jnp.float32)
        dv_ref[span, :] = jnp.zeros((BIG, head_dim), jnp.float32)
        return carry

    lax.fori_loop(0, seq_len // BIG, prepare, 0)

    def wide(row):
        return jnp.broadcast_to(row, (8, tile))

    def fold(block):
        return block.reshape(block.shape[0] // 8, 8, tile)

    def pair(pair_index, carry):
        low_subs = (my_index * half_len + POS * (pair_index + 1) - 1) // SUB + 1

        def geometry(half):
            piece = my_index + half * (last_piece - 2 * my_index)
            bound = piece * half_len + POS * (pair_index + 1)
            full_subs = (bound - 1) // SUB
            row = pl.multiple_of(half * (rows // 2) + pair_index * tile, tile)
            return bound, full_subs // (BIG // SUB), full_subs % (BIG // SUB), half * low_subs * SUB, row

        def score_block(half, key, at, size, row, bound):
            run_max = m_ref[half]
            for sub in range(0, size, SUB):
                scores = _dot(k_ref[pl.ds(key + sub, SUB), :], qt_ref[half])
                if bound is not None and sub + SUB == size:
                    key_pos = key + sub + lax.broadcasted_iota(jnp.int32, (SUB, 1), 0)
                    query_pos = bound - POS + lax.broadcasted_iota(jnp.int32, (1, tile), 1) // heads
                    scores = jnp.where(key_pos <= query_pos, scores, MASK_VALUE)
                strip[pl.ds(at + sub, SUB), :] = scores
                run_max = jnp.maximum(run_max, jnp.max(fold(scores), axis=0))
            m_ref[half] = run_max

        def value_block(half, key, at, size, row, bound):
            run_sum, shift, total = l_ref[half], m_ref[half], None
            for sub in range(0, size, SUB):
                probs = jnp.exp2(fold(strip[pl.ds(at + sub, SUB), :]) * log2_scale - shift[None])
                run_sum = run_sum + jnp.sum(probs, axis=0)
                part = _dot(vt_ref[:, pl.ds(key + sub, SUB)], probs.reshape(SUB, tile).astype(jnp.bfloat16))
                total = part if total is None else total + part
            l_ref[half] = run_sum
            ot_ref[half] += total

        def grad_block(half, key, at, size, row, bound):
            log_sum, d_row, total = m_ref[half], l_ref[half], None
            for sub in range(0, size, SUB):
                span = pl.ds(key + sub, SUB)
                dprobs = _dot(v_ref[span, :], gt_ref[half])
                probs = jnp.exp2(fold(strip[pl.ds(at + sub, SUB), :]) * log2_scale - log_sum[None])
                dscores = probs * (fold(dprobs) - d_row[None])
                probs = probs.reshape(SUB, tile).astype(jnp.bfloat16)
                dscores = dscores.reshape(SUB, tile).astype(jnp.bfloat16)
                dv_ref[span, :] += _dot(probs, g_ref[pl.ds(row, tile), :])
                dk_ref[span, :] += _dot(dscores, q_ref[pl.ds(row, tile), :])
                part = _dot(kt_ref[:, span], dscores)
                total = part if total is None else total + part
            dqt_ref[half] += total

        def sweep(half, block):
            bound, full_steps, rest_subs, start, row = geometry(half)

            def step(index, inner):
                block(half, pl.multiple_of(index * BIG, BIG), pl.multiple_of(start + index * BIG, SUB), BIG, row, None)
                return inner

            lax.fori_loop(0, full_steps, step, 0)
            for count in range(BIG // SUB):

                @pl.when(rest_subs == count)
                def _():
                    key = pl.multiple_of(full_steps * BIG, BIG)
                    block(half, key, pl.multiple_of(start + full_steps * BIG, SUB), (count + 1) * SUB, row, bound)

        def score_pass(half, inner):
            row = geometry(half)[4]
            qt_ref[half] = q_ref[pl.ds(row, tile), :].T
            gt_ref[half] = g_ref[pl.ds(row, tile), :].T
            m_ref[half] = jnp.full((8, tile), MASK_VALUE, jnp.float32)
            sweep(half, score_block)
            return inner

        def value_pass(half, inner):
            row = geometry(half)[4]
            m_ref[half] = wide(jnp.max(m_ref[half], axis=0, keepdims=True) * log2_scale)
            l_ref[half] = jnp.zeros((8, tile), jnp.float32)
            ot_ref[half] = jnp.zeros((head_dim, tile), jnp.float32)
            sweep(half, value_block)
            row_sum = jnp.sum(l_ref[half], axis=0, keepdims=True)
            out = (ot_ref[half] / row_sum).astype(jnp.bfloat16)
            o_ref[pl.ds(row, tile), :] = out.T
            m_ref[half] += wide(jnp.log2(row_sum))
            l_ref[half] = wide(jnp.sum(out.astype(jnp.float32) * gt_ref[half].astype(jnp.float32), axis=0, keepdims=True))
            return inner

        def grad_pass(half, inner):
            row = geometry(half)[4]
            dqt_ref[half] = jnp.zeros((head_dim, tile), jnp.float32)
            sweep(half, grad_block)
            dq_ref[pl.ds(row, tile), :] = (dqt_ref[half] * scale).astype(jnp.bfloat16).T
            return inner

        for one_pass in (score_pass, value_pass, grad_pass):
            lax.fori_loop(0, 2, one_pass, 0)
        return carry

    lax.fori_loop(0, half_len // POS, pair, 0)


def _work_shapes(seq_len, head_dim, tile):
    strip_rows = (seq_len // SUB + 3) * SUB
    return [
        pltpu.VMEM((head_dim, seq_len), jnp.bfloat16),
        pltpu.VMEM((head_dim, seq_len), jnp.bfloat16),
        pltpu.VMEM((strip_rows, tile), jnp.float32),
        pltpu.VMEM((2, head_dim, tile), jnp.bfloat16),
        pltpu.VMEM((2, head_dim, tile), jnp.bfloat16),
        pltpu.VMEM((2, head_dim, tile), jnp.float32),
        pltpu.VMEM((2, head_dim, tile), jnp.float32),
        pltpu.VMEM((2, 8, tile), jnp.float32),
        pltpu.VMEM((2, 8, tile), jnp.float32),
    ]


def _kernel(ctx_size, heads, aliased, q_ref, g_ref, kv_hbm, *rest):
    if aliased:
        rest = rest[2:]
    o_ref, dq_ref, dkv_hbm, k_ref, v_ref, dk_ref, dv_ref, load_sem, store_sem, *work = rest
    step = pl.program_id(0)
    half_len = kv_hbm.shape[3] // 2
    last_piece = 2 * ctx_size - 1

    def pieces(make):
        def each(dev, carry):
            for half in range(2):
                piece = dev + half * (last_piece - 2 * dev)
                there = pl.ds(half * half_len, half_len)
                here = pl.ds(pl.multiple_of(piece * half_len, half_len), half_len)
                for which in range(2):
                    make(dev, which, there, here)
            return carry

        lax.fori_loop(0, ctx_size, each, 0)

    def load(dev, which, there, here):
        pltpu.make_async_copy(kv_hbm.at[dev, step, which, there, :], (k_ref, v_ref)[which].at[here, :], load_sem.at[which]).start()

    def store(dev, which, there, here):
        pltpu.make_async_copy((dk_ref, dv_ref)[which].at[here, :], dkv_hbm.at[dev, step, which, there, :], store_sem.at[which]).start()

    def wait_for(ref, sem):
        pltpu.make_async_copy(ref, ref, sem).wait()

    pieces(load)
    wait_for(k_ref, load_sem.at[0])
    wait_for(v_ref, load_sem.at[1])
    _attention_sequence(lax.axis_index("ctx"), ctx_size, heads, q_ref, g_ref, k_ref, v_ref, o_ref, dq_ref, dk_ref, dv_ref, work)
    pieces(store)
    wait_for(dk_ref, store_sem.at[0])
    wait_for(dv_ref, store_sem.at[1])


def solution(mesh):
    ctx_size = mesh.shape["ctx"]
    block_spec = P("data", "ctx", None, None)

    def local_attention(queries, keys_in, values_in, grad_out):
        batch, shard_len, heads, head_dim = queries.shape
        rows, seq_len, tile = shard_len * heads, shard_len * ctx_size, POS * heads
        group = 2
        q_rows = queries.reshape(batch, rows, head_dim)
        g_rows = grad_out.reshape(batch, rows, head_dim)
        kv_local = jnp.stack([keys_in.reshape(batch, shard_len, head_dim), values_in.reshape(batch, shard_len, head_dim)], axis=1)
        row_shape = jax.ShapeDtypeStruct((batch, rows, head_dim), jnp.bfloat16)
        results = None
        grads = []
        gathered = [lax.all_gather(kv_local[first : first + group], "ctx", axis=0, tiled=False) for first in range(0, batch, group)]
        for part, first in enumerate(range(0, batch, group)):
            row_block = pl.BlockSpec((None, rows, head_dim), lambda step, first=first: (first + step, 0, 0))
            any_spec = pl.BlockSpec(memory_space=pl.ANY)
            operands = [q_rows, g_rows, gathered[part]] + list(results or [])
            out = pl.pallas_call(
                functools.partial(_kernel, ctx_size, heads, results is not None),
                grid=(group,),
                out_shape=[row_shape, row_shape, jax.ShapeDtypeStruct((ctx_size, group, 2, shard_len, head_dim), jnp.float32)],
                in_specs=[row_block, row_block] + [any_spec] * (len(operands) - 2),
                out_specs=[row_block, row_block, any_spec],
                input_output_aliases={3: 0, 4: 1} if results else {},
                scratch_shapes=[
                    pltpu.VMEM((seq_len, head_dim), jnp.bfloat16),
                    pltpu.VMEM((seq_len, head_dim), jnp.bfloat16),
                    pltpu.VMEM((seq_len, head_dim), jnp.float32),
                    pltpu.VMEM((seq_len, head_dim), jnp.float32),
                    pltpu.SemaphoreType.DMA((2,)),
                    pltpu.SemaphoreType.DMA((2,)),
                ]
                + _work_shapes(seq_len, head_dim, tile),
                compiler_params=pltpu.CompilerParams(vmem_limit_bytes=VMEM_BYTES),
                cost_estimate=pl.CostEstimate(flops=2 * 10**10, bytes_accessed=10**8, transcendentals=0),
            )(*operands)
            results = out[:2]
            grads.append(lax.psum_scatter(out[2], "ctx", scatter_dimension=0, tiled=False))
        grad_kv = jnp.concatenate(grads, axis=0)
        grad_k = (grad_kv[:, 0] * head_dim**-0.5).astype(jnp.bfloat16)
        grad_v = grad_kv[:, 1].astype(jnp.bfloat16)
        attn_out = results[0].reshape(queries.shape)
        grad_q = results[1].reshape(queries.shape)
        return attn_out, grad_q, grad_k.reshape(keys_in.shape), grad_v.reshape(values_in.shape)

    return jax.shard_map(local_attention, mesh=mesh, in_specs=(block_spec,) * 4, out_specs=(block_spec,) * 4, check_vma=False)
```

time: 2310 us -> 457 us (0.20)
  matrix products: 770 us -> 0 us
  waiting for transfers between devices: 782 us -> 122 us
  other arithmetic: 334 us -> 5.09 us
  Pallas kernels: 0 us -> 295 us
  local copies, waits for them, and re-layouts: 252 us -> 19.6 us
  starting transfers between devices: 146 us -> 0.78 us
    ppermute x92 -> x0, waiting for transfers between devices: 782 us -> none  [the longest x15 592 us: bwd_step(): k_cur = lax.ppermute(k_cur, 'ctx', perm_next)]
    dot_general x111 -> x0, matrix products: 770 us -> none  [the longest x31 160 us: scores_of(): jnp.einsum('bqhgd,bkhd->bhgqk', q_blk, k_blk, preferred_element_type=jnp....]
    pallas_call x0 -> x3, Pallas kernels: none -> 295 us  [local_attention(): pl.pallas_call(functools.partial(_kernel, ctx_size, heads, results is not...]
    concatenate x43 -> x1, other arithmetic: 229 us -> 1.76 us  [local_attention(): grad_kv = jnp.concatenate(grads, axis=0)]
    ppermute x92 -> x0, starting transfers between devices: 146 us -> none  [the longest x15 95.2 us: fwd_step(): v_cur = lax.ppermute(v_cur, 'ctx', perm_next)]
    slice x30 -> x0, local copies, waits for them, and re-layouts: 110 us -> none  [the longest x14 72.4 us: bwd_future(): dq_acc[:, :half_len]]
    while x76 -> x0, local copies, waits for them, and re-layouts: 107 us -> none
    reduce_sum x16 -> x0, other arithmetic: 81.3 us -> none  [fwd_update(): new_sum = run_sum * decay_factor + jnp.sum(prob_tile, axis=-1)]
  transfers between devices with their start and end apart: 92 -> 6, of which waited for: 48 -> 2; matrix products, arithmetic and copies ran while one was open for 2% -> 4% of each run, Pallas kernels for 0% -> 65%
where the time goes in v1:
time: 457 us; the launch traced here: 456 us
  Pallas kernels  295 us (65%)
  waiting for transfers between devices  122 us (27%)
  local copies, waits for them, and re-layouts  19.6 us (4%)
  between operations  14.2 us (3%)
  other arithmetic  5.09 us (1%)
    pallas_call x3, Pallas kernels, local_attention(): pl.pallas_call(functools.partial(_kernel, ctx_size, heads, results is not...  295 us
    reduce_scatter x3, waiting for transfers between devices, local_attention(): lax.psum_scatter(out[2], 'ctx', scatter_dimension=0, tiled=False)  73.5 us
    all_gather x3, waiting for transfers between devices, local_attention(): lax.all_gather(kv_local[first:first + group], 'ctx', axis=0, tiled=False)  46.9 us
    all_gather x3, local copies, waits for them, and re-layouts, local_attention(): lax.all_gather(kv_local[first:first + group], 'ctx', axis=0, tiled=False)  18.7 us
  transfers between devices with their start and end apart: 6, of which 2 were waited for; matrix products, arithmetic and copies ran while one was open for 4% of the time, Pallas kernels for 65%

profile of v1, /device:TPU:21, one launch (start us, length us, event | category | flops | bytes accessed | tf_op | source)
XLA Modules:
  0.0 456.3 jit_solution(6000984452935838741)
XLA Ops:
  7.2 0.1 all-gather.11.cloned.1.call-start
  7.2 2.4 pad_maximum_fusion.1
  9.6 0.1 all-gather.11.cloned.1.call-update
  9.7 0.1 all-gather.9.cloned.1.call-start
  9.8 0.7 all-gather.9.cloned.1.call-update
  10.5 0.1 all-gather.7.cloned.1.call-start
  10.6 0.7 all-gather.7.cloned.1.call-update
  11.3 0.1 reduce-scatter.4.cloned.1.call-start
  11.4 46.8 %all-gather.11.cloned.1.call-done = bf16[32,2,384,128]{3,2,0,1:T(8,128)(2,1)} async-done(((bf16[2,2,384,128]{3,2,0,1:T(8,128)(2,1)}), bf16[32,2,384,128]{3,2,0,1:T(8,128)(2,1)}) %all-gather.11.cloned.1.call-update) | async-done | bytes 6291472 | tf_op jit(solution)/shard_map/all_gather | solution.py:212
  58.2 6.3 %copy.14 = bf16[32,2,384,128]{3,2,1,0:T(8,128)(2,1)} copy(bf16[32,2,384,128]{3,2,0,1:T(8,128)(2,1)} %all-gather.11.cloned.1.call-done) | data formatting | bytes 12582912 | tf_op jit(solution)/shard_map/all_gather | solution.py:212
  64.5 98.2 %shard_map.75 = (bf16[6,3072,128]{2,1,0:T(8,128)(2,1)}, bf16[6,3072,128]{2,1,0:T(8,128)(2,1)}, f32[16,2,2,384,128]{4,3,2,1,0:T(8,128)}) custom-call(bf16[6,3072,128]{2,1,0:T(8,128)(2,1)} %bitcast.28, bf16[6,3072,128]{2,1,0:T(8,128)(2,1)} %bitcast.31, bf16[16,2,2,384,128]{4,3,2,1,0:T(8,128)(2,1)} %bitcast.22), custom_call_target="tpu_custom_call" | custom-call | flops 20000000000 | bytes 100000000 | tf_op jit(solution)/shard_map/pallas_call | solution.py:217
  162.7 0.1 reduce-scatter.4.cloned.1.call-update
  162.7 0.2 reduce-scatter.6.cloned.1.call-start
  163.0 6.3 %copy.13 = bf16[32,2,384,128]{3,2,1,0:T(8,128)(2,1)} copy(bf16[32,2,384,128]{3,2,0,1:T(8,128)(2,1)} %all-gather.9.cloned.1.call-done) | data formatting | bytes 12582912 | tf_op jit(solution)/shard_map/all_gather | solution.py:212
  169.3 98.2 %shard_map.76 = (bf16[6,3072,128]{2,1,0:T(8,128)(2,1)}, bf16[6,3072,128]{2,1,0:T(8,128)(2,1)}, f32[16,2,2,384,128]{4,3,2,1,0:T(8,128)}) custom-call(bf16[6,3072,128]{2,1,0:T(8,128)(2,1)} %bitcast.29, bf16[6,3072,128]{2,1,0:T(8,128)(2,1)} %bitcast.32, bf16[16,2,2,384,128]{4,3,2,1,0:T(8,128)(2,1)} %bitcast.20, ...), custom_call_target="tpu_custom_call", output_to_operand_aliasing={{0}: (3, {}), {1}: (4, {})} | custom-call | flops 20000000000 | bytes 100000000 | tf_op jit(solution)/shard_map/pallas_call | solution.py:217
  267.4 0.1 reduce-scatter.6.cloned.1.call-update
  267.5 0.3 reduce-scatter.8.cloned.1.call-start
  267.8 6.2 %copy.12 = bf16[32,2,384,128]{3,2,1,0:T(8,128)(2,1)} copy(bf16[32,2,384,128]{3,2,0,1:T(8,128)(2,1)} %all-gather.7.cloned.1.call-done) | data formatting | bytes 12582912 | tf_op jit(solution)/shard_map/all_gather | solution.py:212
  274.0 98.3 %shard_map.77 = (bf16[6,3072,128]{2,1,0:T(8,128)(2,1)}, bf16[6,3072,128]{2,1,0:T(8,128)(2,1)}, f32[16,2,2,384,128]{4,3,2,1,0:T(8,128)}) custom-call(bf16[6,3072,128]{2,1,0:T(8,128)(2,1)} %bitcast.30, bf16[6,3072,128]{2,1,0:T(8,128)(2,1)} %bitcast.33, bf16[16,2,2,384,128]{4,3,2,1,0:T(8,128)(2,1)} %bitcast.21, ...), custom_call_target="tpu_custom_call", output_to_operand_aliasing={{0}: (3, {}), {1}: (4, {})} | custom-call | flops 20000000000 | bytes 100000000 | tf_op jit(solution)/shard_map/pallas_call | solution.py:217
  372.3 0.1 reduce-scatter.8.cloned.1.call-update
  372.4 73.5 %reduce-scatter.8.cloned.1.call-done = f32[1,2,2,384,128]{4,3,2,1,0:T(8,128)} async-done(((f32[16,2,2,384,128]{4,3,2,1,0:T(8,128)}), f32[1,2,2,384,128]{4,3,2,1,0:T(8,128)}) %reduce-scatter.8.cloned.1.call-update) | async-done | bytes 786448 | tf_op jit(solution)/shard_map/reduce_scatter | solution.py:237
  445.9 1.8 pad_maximum_fusion
  447.6 0.9 fusion.2
  448.5 0.9 fusion.1
  (4 shorter events, 0.1 us)
Async XLA Ops:
  7.2 51.0 %all-gather.11.cloned.1.call-start = ((), (), s32[]{:S(2)}) async-start(), calls=%async_computation.8 | async-start | bytes 6684672 | tf_op jit(solution)/shard_map/all_gather | solution.py:212
  9.7 153.3 %all-gather.9.cloned.1.call-start = ((), (), s32[]{:S(2)}) async-start(), calls=%async_computation.7 | async-start | bytes 6684672 | tf_op jit(solution)/shard_map/all_gather | solution.py:212
  10.5 257.3 %all-gather.7.cloned.1.call-start = ((), (), s32[]{:S(2)}) async-start(), calls=%async_computation.6 | async-start | bytes 6684672 | tf_op jit(solution)/shard_map/all_gather | solution.py:212
  11.3 361.0 %reduce-scatter.4.cloned.1.call-start = ((), (), s32[]{:S(2)}) async-start(), calls=%async_computation.3 | async-start | bytes 13369344 | tf_op jit(solution)/shard_map/reduce_scatter | solution.py:237
  162.7 209.7 %reduce-scatter.6.cloned.1.call-start = ((), (), s32[]{:S(2)}) async-start(), calls=%async_computation.4 | async-start | bytes 13369344 | tf_op jit(solution)/shard_map/reduce_scatter | solution.py:237
  267.5 178.4 %reduce-scatter.8.cloned.1.call-start = ((), (), s32[]{:S(2)}) async-start(), calls=%async_computation.5 | async-start | bytes 13369344 | tf_op jit(solution)/shard_map/reduce_scatter | solution.py:237
Sparse Core Ops, SparseCore 0:
  10.2 47.9 all-gather.10
  59.8 41.6 all-gather.8
  103.8 41.4 all-gather.6
  162.8 73.5 reduce-scatter.3
  267.6 73.4 reduce-scatter.5
  372.4 73.3 reduce-scatter.7

commit v2 on v1

--- a/solution.py
+++ b/solution.py
@@ -19,7 +19,7 @@
     return lax.dot_general(lhs, rhs, (((1,), (0,)), ((), ())), preferred_element_type=jnp.float32)
 
 
-def _attention_sequence(my_index, ctx_size, heads, q_ref, g_ref, k_ref, v_ref, o_ref, dq_ref, dk_ref, dv_ref, work):
+def _attention_sequence(my_index, ctx_size, heads, q_ref, g_ref, k_ref, v_ref, o_ref, dq_ref, dk_ref, dv_ref, work, between):
     kt_ref, vt_ref, strip, qt_ref, gt_ref, ot_ref, dqt_ref, m_ref, l_ref = work
     seq_len, head_dim = k_ref.shape
     rows = q_ref.shape[0]
@@ -33,8 +33,6 @@
         span = pl.ds(pl.multiple_of(step * BIG, BIG), BIG)
         kt_ref[:, span] = k_ref[span, :].T
         vt_ref[:, span] = v_ref[span, :].T
-        dk_ref[span, :] = jnp.zeros((BIG, head_dim), jnp.float32)
-        dv_ref[span, :] = jnp.zeros((BIG, head_dim), jnp.float32)
         return carry
 
     lax.fori_loop(0, seq_len // BIG, prepare, 0)
@@ -135,7 +133,8 @@
             dq_ref[pl.ds(row, tile), :] = (dqt_ref[half] * scale).astype(jnp.bfloat16).T
             return inner
 
-        for one_pass in (score_pass, value_pass, grad_pass):
+        for pass_index, one_pass in enumerate((score_pass, value_pass, grad_pass)):
+            between(pair_index, pass_index)
             lax.fori_loop(0, 2, one_pass, 0)
         return carry
 
@@ -157,42 +156,345 @@
     ]
 
 
-def _kernel(ctx_size, heads, aliased, q_ref, g_ref, kv_hbm, *rest):
-    if aliased:
-        rest = rest[2:]
-    o_ref, dq_ref, dkv_hbm, k_ref, v_ref, dk_ref, dv_ref, load_sem, store_sem, *work = rest
-    step = pl.program_id(0)
-    half_len = kv_hbm.shape[3] // 2
+MESH = pl.DeviceIdType.MESH
+STEPS = 9
+
+GATHER_AT = {1: (-1, 1, 2, 3, 5), 2: (3, 5, 6, 8, 10)}
+
+
+def _gather_at(seq):
+    if seq in GATHER_AT:
+        return GATHER_AT[seq]
+    start = STEPS * (seq - 2) - 1
+    return tuple(start + gap for gap in (0, 3, 6, 9, 12))
+
+
+def _kernel(ctx_size, heads, q_hbm, g_hbm, k_hbm, v_hbm, o_hbm, dq_hbm, dk_hbm, dv_hbm, kv_all, *scratch):
+    (
+        qg_buf,
+        od_buf,
+        kv_buf,
+        acc,
+        part,
+        ring_in,
+        out_buf,
+        gather_recv,
+        gather_send,
+        gather_peer_recv,
+        gather_peer_send,
+        load_sem,
+        qg_sem,
+        od_sem,
+        peer_recv,
+        peer_send,
+        ring_recv,
+        ring_send,
+        out_sem,
+        peer_credit,
+        side_credit,
+        *work,
+    ) = scratch
+    batch, shard_len, head_dim = k_hbm.shape
+    half_len = shard_len // 2
+    chips = ctx_size // 2
     last_piece = 2 * ctx_size - 1
-
-    def pieces(make):
+    me = lax.axis_index("ctx")
+    chip, core = me // 2, me % 2
+
+    def device(which_chip, which_core):
+        return lax.rem(which_chip + 2 * chips, chips) * 2 + which_core
+
+    peer = device(chip, 1 - core)
+    sides = (device(chip + 1, core), device(chip - 1, core))
+
+    def remote(src, dst, send_sem, recv_sem, target):
+        return pltpu.make_async_remote_copy(
+            src_ref=src, dst_ref=dst, send_sem=send_sem, recv_sem=recv_sem, device_id={"ctx": target}, device_id_type=MESH
+        )
+
+    def wait_recv(ref, sem, target):
+        remote(ref, ref, sem, sem, target).wait_recv()
+
+    def wait_send(ref, sem, target):
+        remote(ref, ref, sem, sem, target).wait_send()
+
+    def wait_local(ref, sem):
+        pltpu.make_async_copy(ref, ref, sem).wait()
+
+    def gather_send_own(seq):
+        targets = [(sides[way], gather_send.at[way, seq], gather_recv.at[way, seq, 0]) for way in range(2)]
+        targets.append((peer, gather_peer_send.at[seq], gather_peer_recv.at[seq]))
+        for target, send_sem, recv_sem in targets:
+            for which, source in enumerate((k_hbm, v_hbm)):
+                remote(source.at[seq], kv_all.at[seq, 2 * me + which], send_sem, recv_sem, target).start()
+
+    def gather_arrival(seq, hop):
+        far = []
+        for way in range(2):
+            origin = device(chip - hop if way == 0 else chip + hop, core)
+            units = pl.ds(2 * origin, 2) if hop < 4 else pl.ds(2 * origin + way, 1)
+            block = kv_all.at[seq, units]
+            wait_recv(block, gather_recv.at[way, seq, hop - 1], sides[way])
+            if hop < 4:
+                onward = block if hop < 3 else kv_all.at[seq, pl.ds(2 * origin + way, 1)]
+                remote(onward, onward, gather_send.at[way, seq], gather_recv.at[way, seq, hop], sides[way]).start()
+                far.append(block)
+            elif way == 1:
+                far.append(kv_all.at[seq, pl.ds(2 * origin, 2)])
+        for block in far:
+            remote(block, block, gather_peer_send.at[seq], gather_peer_recv.at[seq], peer).start()
+
+    def load_keys(seq):
+        wait_recv(kv_all.at[seq, pl.ds(0, ctx_size)], gather_peer_recv.at[seq], peer)
+        slot = seq % 2
+
         def each(dev, carry):
             for half in range(2):
                 piece = dev + half * (last_piece - 2 * dev)
                 there = pl.ds(half * half_len, half_len)
                 here = pl.ds(pl.multiple_of(piece * half_len, half_len), half_len)
+                for which, own in enumerate((k_hbm, v_hbm)):
+                    target = kv_buf.at[slot, which, here, :]
+
+                    @pl.when(dev == me)
+                    def _():
+                        pltpu.make_async_copy(own.at[seq, there, :], target, load_sem.at[slot]).start()
+
+                    @pl.when(dev != me)
+                    def _():
+                        pltpu.make_async_copy(kv_all.at[seq, 2 * dev + which, there, :], target, load_sem.at[slot]).start()
+
+            return carry
+
+        lax.fori_loop(0, ctx_size, each, 0)
+
+    def piece_rows(dev, half):
+        piece = dev + half * (last_piece - 2 * dev)
+        return pl.ds(pl.multiple_of(piece * half_len, half_len), half_len)
+
+    def reduce_peer_send(seq):
+        slot = seq % 2
+
+        @pl.when(seq >= 2)
+        def _():
+            pl.semaphore_wait(peer_credit, 1)
+
+        def each(where, carry):
+            for half in range(2):
                 for which in range(2):
-                    make(dev, which, there, here)
+                    remote(
+                        acc.at[which, piece_rows(2 * where + 1 - core, half), :],
+                        part.at[slot, 2 * where + which, pl.ds(half * half_len, half_len), :],
+                        peer_send.at[slot],
+                        peer_recv.at[slot],
+                        peer,
+                    ).start()
             return carry
 
-        lax.fori_loop(0, ctx_size, each, 0)
-
-    def load(dev, which, there, here):
-        pltpu.make_async_copy(kv_hbm.at[dev, step, which, there, :], (k_ref, v_ref)[which].at[here, :], load_sem.at[which]).start()
-
-    def store(dev, which, there, here):
-        pltpu.make_async_copy((dk_ref, dv_ref)[which].at[here, :], dkv_hbm.at[dev, step, which, there, :], store_sem.at[which]).start()
-
-    def wait_for(ref, sem):
-        pltpu.make_async_copy(ref, ref, sem).wait()
-
-    pieces(load)
-    wait_for(k_ref, load_sem.at[0])
-    wait_for(v_ref, load_sem.at[1])
-    _attention_sequence(lax.axis_index("ctx"), ctx_size, heads, q_ref, g_ref, k_ref, v_ref, o_ref, dq_ref, dk_ref, dv_ref, work)
-    pieces(store)
-    wait_for(dk_ref, store_sem.at[0])
-    wait_for(dv_ref, store_sem.at[1])
+        lax.fori_loop(0, chips, each, 0)
+
+    def clear_grads():
+        def each(step, carry):
+            for which in range(2):
+                acc[which, pl.ds(pl.multiple_of(step * SUB, SUB), SUB), :] = jnp.zeros((SUB, head_dim), jnp.float32)
+            return carry
+
+        lax.fori_loop(0, acc.shape[1] // SUB, each, 0)
+
+    def ring_chunk(slot, step, way):
+        target = lax.rem(chip + (5 - step if way == 0 else step - 5) + chips, chips)
+        return part.at[slot, pl.ds(2 * target, 2)] if step > 1 else part.at[slot, pl.ds(2 * target + way, 1)]
+
+    def ring_landing(slot, step, way):
+        return ring_in.at[slot, way, pl.ds(2 * (step - 1), 2)] if step > 1 else ring_in.at[slot, way, pl.ds(way, 1)]
+
+    def ring_start(slot, step):
+        for way in range(2):
+            remote(
+                ring_chunk(slot, step, way),
+                ring_landing(slot, step, way),
+                ring_send.at[slot, way],
+                ring_recv.at[slot, way, step - 1],
+                sides[way],
+            ).start()
+
+    def reduce_begin(seq):
+        slot = seq % 2
+        wait_send(part.at[slot], peer_send.at[slot], peer)
+        wait_recv(part.at[slot], peer_recv.at[slot], peer)
+
+        def each(where, carry):
+            for half in range(2):
+                for which in range(2):
+                    place = pl.ds(half * half_len, half_len)
+                    part[slot, 2 * where + which, place, :] += acc[which, piece_rows(2 * where + core, half), :]
+            return carry
+
+        lax.fori_loop(0, chips, each, 0)
+        clear_grads()
+
+        @pl.when(seq >= 2)
+        def _():
+            for way in range(2):
+                pl.semaphore_wait(side_credit.at[way], 1)
+
+        ring_start(slot, 1)
+
+    def reduce_step(seq, step):
+        slot = seq % 2
+        for way in range(2):
+            landing = ring_landing(slot, step - 1, way)
+            wait_recv(landing, ring_recv.at[slot, way, step - 2], sides[way])
+            chunk = ring_chunk(slot, step, way)
+            for unit in range(2) if step > 2 else (way,):
+                chunk[unit] += landing[unit if step > 2 else 0]
+        ring_start(slot, step)
+
+    def reduce_end(seq):
+        slot = seq % 2
+
+        @pl.when(seq >= 2)
+        def _():
+            wait_local(out_buf.at[slot], out_sem.at[slot])
+
+        for way in range(2):
+            wait_recv(ring_landing(slot, 4, way), ring_recv.at[slot, way, 3], sides[way])
+        for which in range(2):
+            total = part[slot, 2 * chip + which] + ring_in[slot, 0, 6 + which] + ring_in[slot, 1, 6 + which]
+            out_buf[slot, which] = (total * (head_dim**-0.5) if which == 0 else total).astype(jnp.bfloat16)
+        for which, target in enumerate((dk_hbm, dv_hbm)):
+            pltpu.make_async_copy(out_buf.at[slot, which], target.at[seq], out_sem.at[slot]).start()
+        for way in range(2):
+            wait_send(ring_in.at[slot, way, pl.ds(0, 7)], ring_send.at[slot, way], sides[way])
+
+        @pl.when(seq + 2 < batch)
+        def _():
+            pl.semaphore_signal(peer_credit, 1, device_id={"ctx": peer}, device_id_type=MESH)
+            for way in range(2):
+                pl.semaphore_signal(side_credit.at[1 - way], 1, device_id={"ctx": sides[way]}, device_id_type=MESH)
+
+    def load_rows(seq):
+        for which, source in enumerate((q_hbm, g_hbm)):
+            pltpu.make_async_copy(source.at[seq], qg_buf.at[seq % 2, which], qg_sem.at[seq % 2]).start()
+
+    load_rows(0)
+    clear_grads()
+    barrier = pltpu.get_barrier_semaphore()
+    for target in (*sides, peer):
+        pl.semaphore_signal(barrier, 1, device_id={"ctx": target}, device_id_type=MESH)
+    pl.semaphore_wait(barrier, 3)
+
+    gather_send_own(0)
+    for hop in range(1, 4):
+        gather_arrival(0, hop)
+    gather_send_own(1)
+    gather_arrival(0, 4)
+    load_keys(0)
+
+    events = [[] for _ in range(STEPS)]
+    for seq in range(1, batch):
+        for hop, at in enumerate(_gather_at(seq)):
+            if at >= 0:
+                events[at % STEPS].append((at // STEPS, functools.partial(gather_send_own, seq) if hop == 0 else functools.partial(gather_arrival, seq, hop)))
+
+    def sequence(seq, carry):
+        slot = seq % 2
+        wait_local(kv_buf.at[slot], load_sem.at[slot])
+        wait_local(qg_buf.at[slot], qg_sem.at[slot])
+
+        @pl.when(seq + 1 < batch)
+        def _():
+            load_rows(seq + 1)
+
+        def between(pair_index, pass_index):
+            for pair in range(STEPS // 3):
+                step = 3 * pair + pass_index
+
+                @pl.when(pair_index == pair)
+                def _():
+                    if step == 0:
+
+                        @pl.when(seq >= 1)
+                        def _():
+                            reduce_peer_send(seq - 1)
+
+                        @pl.when(seq >= 2)
+                        def _():
+                            reduce_step(seq - 2, 4)
+
+                    if step == 1:
+
+                        @pl.when(seq >= 1)
+                        def _():
+                            wait_local(od_buf, od_sem)
+
+                    if step in (2, 4, 6):
+
+                        @pl.when(seq >= 1)
+                        def _():
+                            if step == 2:
+                                reduce_begin(seq - 1)
+                            else:
+                                reduce_step(seq - 1, step // 2)
+
+                    if step == 3:
+
+                        @pl.when(seq >= 2)
+                        def _():
+                            reduce_end(seq - 2)
+
+                    for when, event in events[step]:
+
+                        @pl.when(seq == when)
+                        def _():
+                            event()
+
+                    if step == 6:
+
+                        @pl.when(seq + 1 < batch)
+                        def _():
+                            load_keys(seq + 1)
+
+        _attention_sequence(
+            me,
+            ctx_size,
+            heads,
+            qg_buf.at[slot, 0],
+            qg_buf.at[slot, 1],
+            kv_buf.at[slot, 0],
+            kv_buf.at[slot, 1],
+            od_buf.at[0],
+            od_buf.at[1],
+            acc.at[0],
+            acc.at[1],
+            work,
+            between,
+        )
+        for which, target in enumerate((o_hbm, dq_hbm)):
+            pltpu.make_async_copy(od_buf.at[which], target.at[seq], od_sem).start()
+        return carry
+
+    lax.fori_loop(0, batch, sequence, 0)
+
+    last = batch - 1
+    reduce_peer_send(last)
+    reduce_step(last - 1, 4)
+    reduce_begin(last)
+    reduce_end(last - 1)
+    for step in range(2, 5):
+        reduce_step(last, step)
+    reduce_end(last)
+    wait_local(od_buf, od_sem)
+    for slot in range(2):
+        wait_local(out_buf.at[slot], out_sem.at[slot])
+
+    def drain(seq, carry):
+        for way in range(2):
+            wait_send(kv_all.at[seq, pl.ds(0, 7)], gather_send.at[way, seq], sides[way])
+        wait_send(kv_all.at[seq, pl.ds(0, ctx_size)], gather_peer_send.at[seq], peer)
+        return carry
+
+    lax.fori_loop(0, batch, drain, 0)
 
 
 def solution(mesh):
@@ -202,44 +504,52 @@
     def local_attention(queries, keys_in, values_in, grad_out):
         batch, shard_len, heads, head_dim = queries.shape
         rows, seq_len, tile = shard_len * heads, shard_len * ctx_size, POS * heads
-        group = 2
-        q_rows = queries.reshape(batch, rows, head_dim)
-        g_rows = grad_out.reshape(batch, rows, head_dim)
-        kv_local = jnp.stack([keys_in.reshape(batch, shard_len, head_dim), values_in.reshape(batch, shard_len, head_dim)], axis=1)
         row_shape = jax.ShapeDtypeStruct((batch, rows, head_dim), jnp.bfloat16)
-        results = None
-        grads = []
-        gathered = [lax.all_gather(kv_local[first : first + group], "ctx", axis=0, tiled=False) for first in range(0, batch, group)]
-        for part, first in enumerate(range(0, batch, group)):
-            row_block = pl.BlockSpec((None, rows, head_dim), lambda step, first=first: (first + step, 0, 0))
-            any_spec = pl.BlockSpec(memory_space=pl.ANY)
-            operands = [q_rows, g_rows, gathered[part]] + list(results or [])
-            out = pl.pallas_call(
-                functools.partial(_kernel, ctx_size, heads, results is not None),
-                grid=(group,),
-                out_shape=[row_shape, row_shape, jax.ShapeDtypeStruct((ctx_size, group, 2, shard_len, head_dim), jnp.float32)],
-                in_specs=[row_block, row_block] + [any_spec] * (len(operands) - 2),
-                out_specs=[row_block, row_block, any_spec],
-                input_output_aliases={3: 0, 4: 1} if results else {},
-                scratch_shapes=[
-                    pltpu.VMEM((seq_len, head_dim), jnp.bfloat16),
-                    pltpu.VMEM((seq_len, head_dim), jnp.bfloat16),
-                    pltpu.VMEM((seq_len, head_dim), jnp.float32),
-                    pltpu.VMEM((seq_len, head_dim), jnp.float32),
-                    pltpu.SemaphoreType.DMA((2,)),
-                    pltpu.SemaphoreType.DMA((2,)),
-                ]
-                + _work_shapes(seq_len, head_dim, tile),
-                compiler_params=pltpu.CompilerParams(vmem_limit_bytes=VMEM_BYTES),
-                cost_estimate=pl.CostEstimate(flops=2 * 10**10, bytes_accessed=10**8, transcendentals=0),
-            )(*operands)
-            results = out[:2]
-            grads.append(lax.psum_scatter(out[2], "ctx", scatter_dimension=0, tiled=False))
-        grad_kv = jnp.concatenate(grads, axis=0)
-        grad_k = (grad_kv[:, 0] * head_dim**-0.5).astype(jnp.bfloat16)
-        grad_v = grad_kv[:, 1].astype(jnp.bfloat16)
-        attn_out = results[0].reshape(queries.shape)
-        grad_q = results[1].reshape(queries.shape)
-        return attn_out, grad_q, grad_k.reshape(keys_in.shape), grad_v.reshape(values_in.shape)
+        shard_shape = jax.ShapeDtypeStruct((batch, shard_len, head_dim), jnp.bfloat16)
+        dma, regular = pltpu.SemaphoreType.DMA, pltpu.SemaphoreType.REGULAR
+        attn_out, grad_q, grad_k, grad_v, _ = pl.pallas_call(
+            functools.partial(_kernel, ctx_size, heads),
+            out_shape=[
+                row_shape,
+                row_shape,
+                shard_shape,
+                shard_shape,
+                jax.ShapeDtypeStruct((batch, 2 * ctx_size, shard_len, head_dim), jnp.bfloat16),
+            ],
+            in_specs=[pl.BlockSpec(memory_space=pl.ANY)] * 4,
+            out_specs=[pl.BlockSpec(memory_space=pl.ANY)] * 5,
+            scratch_shapes=[
+                pltpu.VMEM((2, 2, rows, head_dim), jnp.bfloat16),
+                pltpu.VMEM((2, rows, head_dim), jnp.bfloat16),
+                pltpu.VMEM((2, 2, seq_len, head_dim), jnp.bfloat16),
+                pltpu.VMEM((2, seq_len, head_dim), jnp.float32),
+                pltpu.VMEM((2, ctx_size, shard_len, head_dim), jnp.float32),
+                pltpu.VMEM((2, 2, 8, shard_len, head_dim), jnp.float32),
+                pltpu.VMEM((2, 2, shard_len, head_dim), jnp.bfloat16),
+                dma((2, batch, 4)),
+                dma((2, batch)),
+                dma((batch,)),
+                dma((batch,)),
+                dma((2,)),
+                dma((2,)),
+                dma,
+                dma((2,)),
+                dma((2,)),
+                dma((2, 2, 4)),
+                dma((2, 2)),
+                dma((2,)),
+                regular,
+                regular((2,)),
+            ]
+            + _work_shapes(seq_len, head_dim, tile),
+            compiler_params=pltpu.CompilerParams(vmem_limit_bytes=VMEM_BYTES, collective_id=0, has_side_effects=True),
+            cost_estimate=pl.CostEstimate(flops=10**11, bytes_accessed=10**8, transcendentals=0),
+        )(
+            queries.reshape(batch, rows, head_dim),
+            grad_out.reshape(batch, rows, head_dim),
+            keys_in.reshape(batch, shard_len, head_dim),
+            values_in.reshape(batch, shard_len, head_dim),
+        )
+        return attn_out.reshape(queries.shape), grad_q.reshape(queries.shape), grad_k.reshape(keys_in.shape), grad_v.reshape(values_in.shape)
 
     return jax.shard_map(local_attention, mesh=mesh, in_specs=(block_spec,) * 4, out_specs=(block_spec,) * 4, check_vma=False)

time: 457 us -> 364 us (0.80)
  waiting for transfers between devices: 122 us -> 0 us
  Pallas kernels: 295 us -> 353 us
  between operations: 14.2 us -> 0.65 us
  local copies, waits for them, and re-layouts: 19.6 us -> 8.8 us
  other arithmetic: 5.09 us -> 0 us
    reduce_scatter x3 -> x0, waiting for transfers between devices: 73.5 us -> none  [local_attention(): lax.psum_scatter(out[2], 'ctx', scatter_dimension=0, tiled=False)]
    pallas_call x3 -> x1, Pallas kernels: 295 us -> 353 us  [local_attention(): pl.pallas_call(functools.partial(_kernel, ctx_size, heads), out_shape=[ro...]
    all_gather x3 -> x0, waiting for transfers between devices: 46.9 us -> none  [local_attention(): lax.all_gather(kv_local[first:first + group], 'ctx', axis=0, tiled=False)]
    all_gather x3 -> x0, local copies, waits for them, and re-layouts: 18.7 us -> none  [local_attention(): lax.all_gather(kv_local[first:first + group], 'ctx', axis=0, tiled=False)]
    unnamed x1 -> x10, local copies, waits for them, and re-layouts: 0.89 us -> 8.8 us
  transfers between devices with their start and end apart: 6 -> 0, of which waited for: 2 -> 0; matrix products, arithmetic and copies ran while one was open for 4% -> 0% of each run, Pallas kernels for 65% -> 0%
where the time goes in v2:
time: 364 us; the launch traced here: 363 us
  Pallas kernels  353 us (97%)
  local copies, waits for them, and re-layouts  8.8 us (2%)
    pallas_call x1, Pallas kernels, local_attention(): pl.pallas_call(functools.partial(_kernel, ctx_size, heads), out_shape=[ro...  353 us
    unnamed x10, local copies, waits for them, and re-layouts  8.8 us

profile of v2, /device:TPU:21, one launch (start us, length us, event | category | flops | bytes accessed | tf_op | source)
XLA Modules:
  0.0 362.7 jit_solution(9275392387683270450)
XLA Ops:
  0.6 353.2 %shard_map.75 = (bf16[6,3072,128]{2,1,0:T(8,128)(2,1)}, bf16[6,3072,128]{2,1,0:T(8,128)(2,1)}, bf16[6,384,128]{2,1,0:T(8,128)(2,1)}, bf16[6,384,128]{2,1,0:T(8,128)(2,1)}, bf16[6,32,384,128]{3,2,1,0:T(8,128)(2,1)}) custom-call(bf16[6,3072,128]{2,1,0:T(8,128)(2,1)} %bitcast.16, bf16[6,3072,128]{2,1,0:T(8,128)(2,1)} %bitcast.17, ...), custom_call_target="tpu_custom_call" | custom-call | flops 99999997952 | bytes 100000000 | tf_op jit(solution)/shard_map/pallas_call | solution.py:510
  353.9 0.0 copy-start
  353.9 5.0 %copy.14 = bf16[6,384,8,128]{3,2,1,0:T(8,128)(2,1)} copy(bf16[6,384,8,128]{3,2,1,0:T(8,128)(2,1)} %bitcast.13) | data formatting | bytes 9437184
  358.9 0.0 copy-done
  358.9 0.0 copy-start.2
  358.9 0.0 copy-start.1
  358.9 2.2 copy.15
  361.1 0.0 copy-done.2
  361.1 0.8 copy.16
  361.9 0.0 copy-done.1
  361.9 0.8 copy.17
Async XLA Ops:
  353.9 5.0 %copy-start = (bf16[6,3072,128]{2,1,0:T(8,128)(2,1)S(1)}, bf16[6,3072,128]{2,1,0:T(8,128)(2,1)}, u32[]{:S(2)}) copy-start(bf16[6,3072,128]{2,1,0:T(8,128)(2,1)} %get-tuple-element.9) | copy-start | bytes 14155780
  358.9 2.2 copy-start.2
  358.9 3.0 copy-start.1

commit v3 on v2

v3 whole, which is shorter than its diff:
```python
import functools
import math

import jax
import jax.numpy as jnp
from jax import lax
from jax.experimental import pallas as pl
from jax.experimental.pallas import tpu as pltpu
from jax.sharding import PartitionSpec as P

MASK_VALUE = -1e30
BIG = 1024
SUB = 256
POS = 64
VMEM_BYTES = 60 * 2**20


def _dot_first(lhs, rhs):
    return lax.dot_general(lhs, rhs, (((0,), (0,)), ((), ())), preferred_element_type=jnp.float32)


def _dot(lhs, rhs):
    return lax.dot_general(lhs, rhs, (((1,), (0,)), ((), ())), preferred_element_type=jnp.float32)


def _attention_sequence(my_index, ctx_size, heads, q_ref, g_ref, k_ref, v_ref, o_ref, dq_ref, dk_ref, dv_ref, work, between):
    strip, recent, qt_ref, gt_ref, ot_ref, dqt_ref, max_ref, used_max_ref, sum_ref = work
    head_dim = k_ref.shape[1]
    rows = q_ref.shape[0]
    half_len = rows // heads // 2
    tile = POS * heads
    subs = BIG // SUB
    scale = head_dim**-0.5
    log2_scale = scale * math.log2(math.e)
    last_piece = 2 * ctx_size - 1

    def wide(row):
        return jnp.broadcast_to(row, (8, tile))

    def top(partial):
        return wide(jnp.max(partial, axis=0, keepdims=True)) * log2_scale

    def fold(block):
        return block.reshape(block.shape[0] // 8, 8, tile)

    def add(total, part):
        return part if total is None else total + part

    def pair(pair_index, carry):
        low_subs = (my_index * half_len + POS * (pair_index + 1) - 1) // SUB + 1

        def geometry(half):
            piece = my_index + half * (last_piece - 2 * my_index)
            bound = piece * half_len + POS * (pair_index + 1)
            full_subs = (bound - 1) // SUB
            row = pl.multiple_of(half * (rows // 2) + pair_index * tile, tile)
            return bound, full_subs // subs, full_subs % subs, half * low_subs * SUB, row

        def score(half, key, at, sub, partial, bound=None):
            scores = _dot(k_ref[pl.ds(key, SUB), :], qt_ref[half])
            if bound is not None:
                key_pos = key + lax.broadcasted_iota(jnp.int32, (SUB, 1), 0)
                query_pos = bound - POS + lax.broadcasted_iota(jnp.int32, (1, tile), 1) // heads
                scores = jnp.where(key_pos <= query_pos, scores, MASK_VALUE)
            strip[pl.ds(at, SUB), :] = scores
            recent[sub * SUB : (sub + 1) * SUB, :] = scores
            return jnp.maximum(partial, jnp.max(fold(scores), axis=0))

        def value(key, sub, shift, run_sum, total):
            probs = jnp.exp2(fold(recent[sub * SUB : (sub + 1) * SUB, :]) * log2_scale - shift[None])
            part = _dot_first(v_ref[pl.ds(key, SUB), :], probs.reshape(SUB, tile).astype(jnp.bfloat16))
            return run_sum + jnp.sum(probs, axis=0), add(total, part)

        def rescaled(half, total, decay):
            ot_ref[half] = (fold(ot_ref[half]) * decay[None]).reshape(head_dim, tile) + total

        def forward_pass(half, inner):
            bound, full_steps, rest_subs, start, row = geometry(half)
            qt_ref[half] = q_ref[pl.ds(row, tile), :].T
            gt_ref[half] = g_ref[pl.ds(row, tile), :].T
            lowest = jnp.full((8, tile), MASK_VALUE, jnp.float32)
            for count in range(subs):

                @pl.when(rest_subs == count)
                def _():
                    key, at = pl.multiple_of(full_steps * BIG, BIG), pl.multiple_of(start, SUB)
                    partial = lowest
                    for sub in range(count + 1):
                        partial = score(half, key + sub * SUB, at + sub * SUB, sub, partial, bound if sub == count else None)
                    shift = top(partial)
                    run_sum, total, ahead = jnp.zeros((8, tile), jnp.float32), None, partial
                    for sub in range(subs):
                        if sub <= count:
                            run_sum, total = value(key + sub * SUB, sub, shift, run_sum, total)
                        ahead = score(half, sub * SUB, at + (count + 1 + sub) * SUB, sub, ahead)
                    ot_ref[half] = total
                    sum_ref[half] = run_sum
                    used_max_ref[half] = shift
                    max_ref[half] = jnp.where(full_steps > 0, top(ahead), shift)

            def step(index, last):
                key = pl.multiple_of((index - 1) * BIG, BIG)
                at = pl.multiple_of(start + (rest_subs + 1) * SUB + index * BIG, SUB)
                shift = max_ref[half]
                decay = jnp.exp2(used_max_ref[half] - shift)
                run_sum, total, partial = sum_ref[half] * decay, None, lowest
                for sub in range(subs):
                    run_sum, total = value(key + sub * SUB, sub, shift, run_sum, total)
                    if not last:
                        partial = score(half, key + BIG + sub * SUB, at + sub * SUB, sub, partial)
                sum_ref[half] = run_sum
                rescaled(half, total, decay)
                used_max_ref[half] = shift
                if not last:
                    max_ref[half] = jnp.maximum(shift, top(partial))

            def inner_step(index, carry):
                step(index, False)
                return carry

            lax.fori_loop(1, full_steps, inner_step, 0)

            @pl.when(full_steps > 0)
            def _():
                step(full_steps, True)

            row_sum = jnp.sum(sum_ref[half], axis=0, keepdims=True)
            out = (ot_ref[half] / row_sum).astype(jnp.bfloat16)
            o_ref[pl.ds(row, tile), :] = out.T
            max_ref[half] = used_max_ref[half] + wide(jnp.log2(row_sum))
            sum_ref[half] = wide(jnp.sum(out.astype(jnp.float32) * gt_ref[half].astype(jnp.float32), axis=0, keepdims=True))
            return inner

        def grad(half, key, at, size, row):
            log_sum, d_row, total = max_ref[half], sum_ref[half], None
            for sub in range(0, size, SUB):
                span = pl.ds(key + sub, SUB)
                dprobs = _dot(v_ref[span, :], gt_ref[half])
                probs = jnp.exp2(fold(strip[pl.ds(at + sub, SUB), :]) * log2_scale - log_sum[None])
                dscores = probs * (fold(dprobs) - d_row[None])
                probs = probs.reshape(SUB, tile).astype(jnp.bfloat16)
                dscores = dscores.reshape(SUB, tile).astype(jnp.bfloat16)
                dv_ref[span, :] += _dot(probs, g_ref[pl.ds(row, tile), :])
                dk_ref[span, :] += _dot(dscores, q_ref[pl.ds(row, tile), :])
                total = add(total, _dot_first(k_ref[span, :], dscores))
            dqt_ref[half] += total

        def backward_pass(half, inner):
            bound, full_steps, rest_subs, start, row = geometry(half)
            main = start + (rest_subs + 1) * SUB
            dqt_ref[half] = jnp.zeros((head_dim, tile), jnp.float32)

            def step(index, carry):
                key = pl.multiple_of(index * 2 * BIG, BIG)
                grad(half, key, pl.multiple_of(main + key, SUB), 2 * BIG, row)
                return carry

            lax.fori_loop(0, full_steps // 2, step, 0)

            @pl.when(full_steps % 2 == 1)
            def _():
                key = pl.multiple_of((full_steps - 1) * BIG, BIG)
                grad(half, key, pl.multiple_of(main + key, SUB), BIG, row)

            for count in range(subs):

                @pl.when(rest_subs == count)
                def _():
                    grad(half, pl.multiple_of(full_steps * BIG, BIG), pl.multiple_of(start, SUB), (count + 1) * SUB, row)

            dq_ref[pl.ds(row, tile), :] = (dqt_ref[half] * scale).astype(jnp.bfloat16).T
            return inner

        for pass_index, one_pass in enumerate((forward_pass, backward_pass)):
            between(pair_index, pass_index)
            lax.fori_loop(0, 2, one_pass, 0)
        return carry

    lax.fori_loop(0, half_len // POS, pair, 0)


def _work_shapes(seq_len, head_dim, tile):
    strip_rows = (seq_len // SUB + 3 + BIG // SUB) * SUB
    return [
        pltpu.VMEM((strip_rows, tile), jnp.float32),
        pltpu.VMEM((BIG, tile), jnp.float32),
        pltpu.VMEM((2, head_dim, tile), jnp.bfloat16),
        pltpu.VMEM((2, head_dim, tile), jnp.bfloat16),
        pltpu.VMEM((2, head_dim, tile), jnp.float32),
        pltpu.VMEM((2, head_dim, tile), jnp.float32),
        pltpu.VMEM((2, 8, tile), jnp.float32),
        pltpu.VMEM((2, 8, tile), jnp.float32),
        pltpu.VMEM((2, 8, tile), jnp.float32),
    ]


MESH = pl.DeviceIdType.MESH
SLOTS = 6

GATHER_AT = {1: (-1, 1, 3, 4, 5), 2: (0, 2, 4, 7, 9), 3: (1, 5, 8, 10, 13), 4: (11, 14, 17, 18, 21)}


def _gather_at(seq):
    if seq in GATHER_AT:
        return GATHER_AT[seq]
    return tuple(SLOTS * (seq - 2) + gap for gap in (2, 4, 6, 8, 10))


def _kernel(ctx_size, heads, q_hbm, g_hbm, k_hbm, v_hbm, o_hbm, dq_hbm, dk_hbm, dv_hbm, kv_all, *scratch):
    (
        qg_buf,
        od_buf,
        kv_buf,
        acc,
        part,
        ring_in,
        out_buf,
        gather_recv,
        gather_send,
        gather_peer_recv,
        gather_peer_send,
        load_sem,
        qg_sem,
        od_sem,
        peer_recv,
        peer_send,
        ring_recv,
        ring_send,
        out_sem,
        peer_credit,
        side_credit,
        *work,
    ) = scratch
    batch, shard_len, head_dim = k_hbm.shape
    half_len = shard_len // 2
    chips = ctx_size // 2
    last_piece = 2 * ctx_size - 1
    me = lax.axis_index("ctx")
    chip, core = me // 2, me % 2

    def device(which_chip, which_core):
        return lax.rem(which_chip + 2 * chips, chips) * 2 + which_core

    peer = device(chip, 1 - core)
    sides = (device(chip + 1, core), device(chip - 1, core))

    def remote(src, dst, send_sem, recv_sem, target):
        return pltpu.make_async_remote_copy(
            src_ref=src, dst_ref=dst, send_sem=send_sem, recv_sem=recv_sem, device_id={"ctx": target}, device_id_type=MESH
        )

    def wait_recv(ref, sem, target):
        remote(ref, ref, sem, sem, target).wait_recv()

    def wait_send(ref, sem, target):
        remote(ref, ref, sem, sem, target).wait_send()

    def wait_local(ref, sem):
        pltpu.make_async_copy(ref, ref, sem).wait()

    def piece_rows(dev, half):
        piece = dev + half * (last_piece - 2 * dev)
        return pl.ds(pl.multiple_of(piece * half_len, half_len), half_len)

    def shard_refs(seq, dev, which):
        if seq == 0:
            return [kv_buf.at[0, which, piece_rows(dev, half), :] for half in range(2)]
        return [kv_all.at[seq, 2 * dev + which]]

    def send_shard(sources, seq, dev, which, targets):
        for target, send_sem, recv_sem in targets:
            for source, place in zip(sources, shard_refs(seq, dev, which)):
                remote(source, place, send_sem, recv_sem, target).start()

    def to_side(way, seq, which, hop):
        return sides[way], gather_send.at[way, seq], gather_recv.at[way, which, seq, hop]

    def to_peer(seq):
        return peer, gather_peer_send.at[seq], gather_peer_recv.at[seq]

    def gather_send_own(seq):
        for which, source in enumerate((k_hbm, v_hbm)):
            sources = [source.at[seq]]
            if seq == 0:
                sources = [source.at[seq, pl.ds(half * half_len, half_len), :] for half in range(2)]
            send_shard(sources, seq, me, which, [to_side(0, seq, which, 0), to_side(1, seq, which, 0), to_peer(seq)])

    def gather_arrival(seq, hop):
        for which in range(2):
            for way in range(2) if hop < 4 else (which,):
                origin = device(chip - hop if way == 0 else chip + hop, core)
                refs = shard_refs(seq, origin, which)
                wait_recv(kv_all.at[0, 0], gather_recv.at[way, which, seq, hop - 1], sides[way])
                onward = [to_side(way, seq, which, hop)] if hop < (4 if way == which else 3) else []
                send_shard(refs, seq, origin, which, onward + [to_peer(seq)])

    def drain(seq, carry):
        for way in range(2):
            wait_send(kv_all.at[0, pl.ds(0, 7)], gather_send.at[way, seq], sides[way])
        wait_send(kv_all.at[0, pl.ds(0, ctx_size)], gather_peer_send.at[seq], peer)
        return carry

    def load_keys(seq):
        wait_recv(kv_all.at[seq, pl.ds(0, ctx_size)], gather_peer_recv.at[seq], peer)
        slot = seq % 2

        def each(dev, carry):
            for half in range(2):
                piece = dev + half * (last_piece - 2 * dev)
                there = pl.ds(half * half_len, half_len)
                here = pl.ds(pl.multiple_of(piece * half_len, half_len), half_len)
                for which, own in enumerate((k_hbm, v_hbm)):
                    target = kv_buf.at[slot, which, here, :]

                    @pl.when(dev == me)
                    def _():
                        pltpu.make_async_copy(own.at[seq, there, :], target, load_sem.at[slot]).start()

                    @pl.when(dev != me)
                    def _():
                        pltpu.make_async_copy(kv_all.at[seq, 2 * dev + which, there, :], target, load_sem.at[slot]).start()

            return carry

        lax.fori_loop(0, ctx_size, each, 0)

    chunk_order = (chips // 2, chips // 2 - 1, chips // 2 + 1, chips // 2 - 2, chips // 2 + 2, 1, chips - 1, 0)

    def chunk_chip(offset):
        return lax.rem(chip + offset, chips)

    def reduce_peer_send(seq):
        slot = seq % 2

        @pl.when(seq >= 2)
        def _():
            pl.semaphore_wait(peer_credit, 1)

        for index, offset in enumerate(chunk_order):
            where = chunk_chip(offset)
            for half in range(2):
                for which in range(2):
                    remote(
                        acc.at[which, piece_rows(2 * where + 1 - core, half), :],
                        part.at[slot, 2 * where + which, pl.ds(half * half_len, half_len), :],
                        peer_send.at[slot],
                        peer_recv.at[slot, index],
                        peer,
                    ).start()

    def clear_grads():
        def each(step, carry):
            for which in range(2):
                acc[which, pl.ds(pl.multiple_of(step * SUB, SUB), SUB), :] = jnp.zeros((SUB, head_dim), jnp.float32)
            return carry

        lax.fori_loop(0, acc.shape[1] // SUB, each, 0)

    def ring_chunk(slot, step, way, which):
        return part.at[slot, 2 * chunk_chip(5 - step if way == 0 else chips - 5 + step) + which]

    def ring_send_step(slot, step, way, which):
        remote(
            ring_chunk(slot, step, way, which),
            ring_in.at[slot, way, which, step - 1],
            ring_send.at[slot, way],
            ring_recv.at[slot, way, which, step - 1],
            sides[way],
        ).start()

    def ring_wait(slot, step, way, which):
        wait_recv(ring_in.at[slot, way, which, step - 1], ring_recv.at[slot, way, which, step - 1], sides[way])

    def reduce_begin(seq):
        slot = seq % 2

        @pl.when(seq >= 2)
        def _():
            for way in range(2):
                pl.semaphore_wait(side_credit.at[way], 1)

        for index, offset in enumerate(chunk_order):
            where = chunk_chip(offset)
            wait_recv(part.at[slot, pl.ds(2 * where, 2)], peer_recv.at[slot, index], peer)
            for half in range(2):
                for which in range(2):
                    place = pl.ds(half * half_len, half_len)
                    part[slot, 2 * where + which, place, :] += acc[which, piece_rows(2 * where + core, half), :]
            if index == 0:
                for way in range(2):
                    ring_send_step(slot, 1, way, way)
            elif index < 3:
                ring_send_step(slot, 2, index - 1, 2 - index)
        wait_send(part.at[slot], peer_send.at[slot], peer)
        clear_grads()

    def reduce_step(seq, step, long_chain):
        slot = seq % 2
        for way in range(2):
            which = way if long_chain else 1 - way
            ring_wait(slot, step - 1, way, which)
            ring_chunk(slot, step, way, which)[...] += ring_in[slot, way, which, step - 2]
        for way in range(2):
            ring_send_step(slot, step, way, way if long_chain else 1 - way)

    def reduce_end(seq):
        slot = seq % 2

        @pl.when(seq >= 2)
        def _():
            wait_local(out_buf.at[slot], out_sem.at[slot])

        for which, target in enumerate((dk_hbm, dv_hbm)):
            for way in (1 - which, which):
                ring_wait(slot, 4, way, which)
            total = part[slot, 2 * chip + which] + ring_in[slot, 0, which, 3] + ring_in[slot, 1, which, 3]
            out_buf[slot, which] = (total * (head_dim**-0.5) if which == 0 else total).astype(jnp.bfloat16)
            pltpu.make_async_copy(out_buf.at[slot, which], target.at[seq], out_sem.at[slot]).start()
        for way in range(2):
            wait_send(part.at[slot, pl.ds(0, 7)], ring_send.at[slot, way], sides[way])

        @pl.when(seq + 2 < batch)
        def _():
            pl.semaphore_signal(peer_credit, 1, device_id={"ctx": peer}, device_id_type=MESH)
            for way in range(2):
                pl.semaphore_signal(side_credit.at[1 - way], 1, device_id={"ctx": sides[way]}, device_id_type=MESH)

    def load_rows(seq):
        for which, source in enumerate((q_hbm, g_hbm)):
            pltpu.make_async_copy(source.at[seq], qg_buf.at[seq % 2, which], qg_sem.at[seq % 2]).start()

    load_rows(0)
    clear_grads()
    barrier = pltpu.get_barrier_semaphore()
    for target in (*sides, peer):
        pl.semaphore_signal(barrier, 1, device_id={"ctx": target}, device_id_type=MESH)
    pl.semaphore_wait(barrier, 3)

    gather_send_own(0)
    own_loads = [
        pltpu.make_async_copy(source.at[0, pl.ds(half * half_len, half_len), :], place, load_sem.at[0])
        for which, source in enumerate((k_hbm, v_hbm))
        for half, place in enumerate(shard_refs(0, me, which))
    ]
    for copy in own_loads:
        copy.start()
    for hop in range(1, 4):
        gather_arrival(0, hop)
    gather_send_own(1)
    gather_arrival(0, 4)
    wait_recv(kv_all.at[0, pl.ds(0, ctx_size)], gather_peer_recv.at[0], peer)
    wait_local(kv_all.at[0, pl.ds(0, 2)], load_sem.at[0])

    events = [[] for _ in range(SLOTS)]
    for seq in range(1, batch):
        for hop, at in enumerate(_gather_at(seq)):
            if at >= 0:
                event = functools.partial(gather_arrival, seq, hop) if hop else functools.partial(gather_send_own, seq)
                events[at % SLOTS].append((at // SLOTS, event))

    events[0].append((1, functools.partial(drain, 0, 0)))

    def steps(*which):
        return lambda seq: [reduce_step(seq, *one) for one in which]

    last = batch - 1
    reduce_events = {
        (0, 1): reduce_peer_send,
        (1, 1): reduce_begin,
        (3, 1): steps((2, True), (3, False)),
        (4, 1): steps((3, True)),
        (5, 1): steps((4, False)),
        (0, 2): steps((4, True)),
        (3, 2): reduce_end,
    }
    last_events = {
        (0, 1): reduce_peer_send,
        (1, 1): reduce_begin,
        (2, 1): steps((2, True)),
        (3, 1): steps((3, False), (3, True)),
        (5, 1): steps((4, False), (4, True)),
        (0, 2): reduce_events[0, 2],
        (3, 2): reduce_end,
    }

    def sequence(seq, carry):
        slot = seq % 2

        @pl.when(seq >= 1)
        def _():
            wait_local(kv_buf.at[slot], load_sem.at[slot])

        wait_local(qg_buf.at[slot], qg_sem.at[slot])

        @pl.when(seq >= 2)
        def _():
            wait_local(od_buf.at[slot], od_sem.at[slot])

        @pl.when(seq + 1 < batch)
        def _():
            load_rows(seq + 1)

        def between(pair_index, pass_index):
            for pair in range(SLOTS // 2):
                at = 2 * pair + pass_index

                @pl.when(pair_index == pair)
                def _():
                    for when, event in events[at]:

                        @pl.when(seq == when)
                        def _():
                            event()

                    for lag in (2, 1):
                        usual, final = reduce_events.get((at, lag)), last_events.get((at, lag))
                        if usual and usual is final:

                            @pl.when(seq >= lag)
                            def _():
                                usual(seq - lag)

                        elif usual or final:

                            @pl.when((seq >= lag) & (seq < last))
                            def _():
                                if usual:
                                    usual(seq - lag)

                            @pl.when(seq == last)
                            def _():
                                if final:
                                    final(seq - lag)

                    if at == SLOTS - 1:

                        @pl.when(seq + 1 < batch)
                        def _():
                            load_keys(seq + 1)

        _attention_sequence(
            me,
            ctx_size,
            heads,
            qg_buf.at[slot, 0],
            qg_buf.at[slot, 1],
            kv_buf.at[slot, 0],
            kv_buf.at[slot, 1],
            od_buf.at[slot, 0],
            od_buf.at[slot, 1],
            acc.at[0],
            acc.at[1],
            work,
            between,
        )
        for which, target in enumerate((o_hbm, dq_hbm)):
            pltpu.make_async_copy(od_buf.at[slot, which], target.at[seq], od_sem.at[slot]).start()
        return carry

    lax.fori_loop(0, batch, sequence, 0)

    reduce_peer_send(last)
    reduce_begin(last)
    reduce_step(last, 2, True)
    reduce_end(last - 1)
    for step in range(3, 5):
        reduce_step(last, step, False)
        reduce_step(last, step, True)
    reduce_end(last)
    for slot in range(2):
        wait_local(od_buf.at[slot], od_sem.at[slot])
        wait_local(out_buf.at[slot], out_sem.at[slot])

    lax.fori_loop(1, batch, drain, 0)


def solution(mesh):
    ctx_size = mesh.shape["ctx"]
    block_spec = P("data", "ctx", None, None)

    def local_attention(queries, keys_in, values_in, grad_out):
        batch, shard_len, heads, head_dim = queries.shape
        rows, seq_len, tile = shard_len * heads, shard_len * ctx_size, POS * heads
        row_shape = jax.ShapeDtypeStruct((batch, rows, head_dim), jnp.bfloat16)
        shard_shape = jax.ShapeDtypeStruct((batch, shard_len, head_dim), jnp.bfloat16)
        dma, regular = pltpu.SemaphoreType.DMA, pltpu.SemaphoreType.REGULAR
        attn_out, grad_q, grad_k, grad_v, _ = pl.pallas_call(
            functools.partial(_kernel, ctx_size, heads),
            out_shape=[
                row_shape,
                row_shape,
                shard_shape,
                shard_shape,
                jax.ShapeDtypeStruct((batch, 2 * ctx_size, shard_len, head_dim), jnp.bfloat16),
            ],
            in_specs=[pl.BlockSpec(memory_space=pl.ANY)] * 4,
            out_specs=[pl.BlockSpec(memory_space=pl.ANY)] * 5,
            scratch_shapes=[
                pltpu.VMEM((2, 2, rows, head_dim), jnp.bfloat16),
                pltpu.VMEM((2, 2, rows, head_dim), jnp.bfloat16),
                pltpu.VMEM((2, 2, seq_len, head_dim), jnp.bfloat16),
                pltpu.VMEM((2, seq_len, head_dim), jnp.float32),
                pltpu.VMEM((2, ctx_size, shard_len, head_dim), jnp.float32),
                pltpu.VMEM((2, 2, 2, 4, shard_len, head_dim), jnp.float32),
                pltpu.VMEM((2, 2, shard_len, head_dim), jnp.bfloat16),
                dma((2, 2, batch, 4)),
                dma((2, batch)),
                dma((batch,)),
                dma((batch,)),
                dma((2,)),
                dma((2,)),
                dma((2,)),
                dma((2, ctx_size // 2)),
                dma((2,)),
                dma((2, 2, 2, 4)),
                dma((2, 2)),
                dma((2,)),
                regular,
                regular((2,)),
            ]
            + _work_shapes(seq_len, head_dim, tile),
            compiler_params=pltpu.CompilerParams(vmem_limit_bytes=VMEM_BYTES, collective_id=0, has_side_effects=True),
            cost_estimate=pl.CostEstimate(flops=10**11, bytes_accessed=10**8, transcendentals=0),
        )(
            queries.reshape(batch, rows, head_dim),
            grad_out.reshape(batch, rows, head_dim),
            keys_in.reshape(batch, shard_len, head_dim),
            values_in.reshape(batch, shard_len, head_dim),
        )
        return attn_out.reshape(queries.shape), grad_q.reshape(queries.shape), grad_k.reshape(keys_in.shape), grad_v.reshape(values_in.shape)

    return jax.shard_map(local_attention, mesh=mesh, in_specs=(block_spec,) * 4, out_specs=(block_spec,) * 4, check_vma=False)
```

time: 364 us -> 322 us (0.88)
  Pallas kernels: 353 us -> 312 us
    pallas_call x1, Pallas kernels: 353 us -> 312 us  [local_attention(): pl.pallas_call(functools.partial(_kernel, ctx_size, heads), out_shape=[ro...]
where the time goes in v3:
time: 322 us
  Pallas kernels  312 us (97%)
  local copies, waits for them, and re-layouts  8.8 us (3%)
    pallas_call x1, Pallas kernels, local_attention(): pl.pallas_call(functools.partial(_kernel, ctx_size, heads), out_shape=[ro...  312 us
    unnamed x10, local copies, waits for them, and re-layouts  8.8 us

profile of v3, /device:TPU:21, one launch (start us, length us, event | category | flops | bytes accessed | tf_op | source)
XLA Modules:
  0.0 321.9 jit_solution(2087066110428970296)
XLA Ops:
  0.6 312.4 %shard_map.75 = (bf16[6,3072,128]{2,1,0:T(8,128)(2,1)}, bf16[6,3072,128]{2,1,0:T(8,128)(2,1)}, bf16[6,384,128]{2,1,0:T(8,128)(2,1)}, bf16[6,384,128]{2,1,0:T(8,128)(2,1)}, bf16[6,32,384,128]{3,2,1,0:T(8,128)(2,1)}) custom-call(bf16[6,3072,128]{2,1,0:T(8,128)(2,1)} %bitcast.16, bf16[6,3072,128]{2,1,0:T(8,128)(2,1)} %bitcast.17, ...), custom_call_target="tpu_custom_call" | custom-call | flops 99999997952 | bytes 100000000 | tf_op jit(solution)/shard_map/pallas_call | solution.py:587
  313.1 0.0 copy-start
  313.1 5.0 %copy.14 = bf16[6,384,8,128]{3,2,1,0:T(8,128)(2,1)} copy(bf16[6,384,8,128]{3,2,1,0:T(8,128)(2,1)} %bitcast.13) | data formatting | bytes 9437184
  318.1 0.0 copy-done
  318.1 0.0 copy-start.2
  318.1 0.0 copy-start.1
  318.1 2.2 copy.15
  320.3 0.0 copy-done.2
  320.3 0.8 copy.16
  321.1 0.0 copy-done.1
  321.1 0.8 copy.17
Async XLA Ops:
  313.1 5.0 %copy-start = (bf16[6,3072,128]{2,1,0:T(8,128)(2,1)S(1)}, bf16[6,3072,128]{2,1,0:T(8,128)(2,1)}, u32[]{:S(2)}) copy-start(bf16[6,3072,128]{2,1,0:T(8,128)(2,1)} %get-tuple-element.9) | copy-start | bytes 14155780
  318.1 2.2 copy-start.2
  318.1 3.0 copy-start.1

commit v4 on v3

--- a/solution.py
+++ b/solution.py
@@ -56,28 +56,27 @@
             row = pl.multiple_of(half * (rows // 2) + pair_index * tile, tile)
             return bound, full_subs // subs, full_subs % subs, half * low_subs * SUB, row
 
-        def score(half, key, at, sub, partial, bound=None):
+        def score(half, key, at, sub, partial, bound=None, into=0):
             scores = _dot(k_ref[pl.ds(key, SUB), :], qt_ref[half])
             if bound is not None:
                 key_pos = key + lax.broadcasted_iota(jnp.int32, (SUB, 1), 0)
                 query_pos = bound - POS + lax.broadcasted_iota(jnp.int32, (1, tile), 1) // heads
                 scores = jnp.where(key_pos <= query_pos, scores, MASK_VALUE)
             strip[pl.ds(at, SUB), :] = scores
-            recent[sub * SUB : (sub + 1) * SUB, :] = scores
+            recent[into, sub * SUB : (sub + 1) * SUB, :] = scores
             return jnp.maximum(partial, jnp.max(fold(scores), axis=0))
 
-        def value(key, sub, shift, run_sum, total):
-            probs = jnp.exp2(fold(recent[sub * SUB : (sub + 1) * SUB, :]) * log2_scale - shift[None])
-            part = _dot_first(v_ref[pl.ds(key, SUB), :], probs.reshape(SUB, tile).astype(jnp.bfloat16))
-            return run_sum + jnp.sum(probs, axis=0), add(total, part)
+        def weights(sub, shift, source=0):
+            return jnp.exp2(fold(recent[source, sub * SUB : (sub + 1) * SUB, :]) * log2_scale - shift[None])
+
+        def value(key, probs, total):
+            return add(total, _dot_first(v_ref[pl.ds(key, SUB), :], probs.reshape(SUB, tile).astype(jnp.bfloat16)))
 
         def rescaled(half, total, decay):
             ot_ref[half] = (fold(ot_ref[half]) * decay[None]).reshape(head_dim, tile) + total
 
         def forward_pass(half, inner):
             bound, full_steps, rest_subs, start, row = geometry(half)
-            qt_ref[half] = q_ref[pl.ds(row, tile), :].T
-            gt_ref[half] = g_ref[pl.ds(row, tile), :].T
             lowest = jnp.full((8, tile), MASK_VALUE, jnp.float32)
             for count in range(subs):
 
@@ -86,13 +85,14 @@
                     key, at = pl.multiple_of(full_steps * BIG, BIG), pl.multiple_of(start, SUB)
                     partial = lowest
                     for sub in range(count + 1):
-                        partial = score(half, key + sub * SUB, at + sub * SUB, sub, partial, bound if sub == count else None)
-                    shift = top(partial)
-                    run_sum, total, ahead = jnp.zeros((8, tile), jnp.float32), None, partial
+                        partial = score(half, key + sub * SUB, at + sub * SUB, sub, partial, bound if sub == count else None, 1)
+                    shift, ahead = top(partial), partial
                     for sub in range(subs):
-                        if sub <= count:
-                            run_sum, total = value(key + sub * SUB, sub, shift, run_sum, total)
                         ahead = score(half, sub * SUB, at + (count + 1 + sub) * SUB, sub, ahead)
+                    run_sum, total = jnp.zeros((8, tile), jnp.float32), None
+                    for sub in range(count + 1):
+                        probs = weights(sub, shift, 1)
+                        run_sum, total = run_sum + jnp.sum(probs, axis=0), value(key + sub * SUB, probs, total)
                     ot_ref[half] = total
                     sum_ref[half] = run_sum
                     used_max_ref[half] = shift
@@ -105,9 +105,11 @@
                 decay = jnp.exp2(used_max_ref[half] - shift)
                 run_sum, total, partial = sum_ref[half] * decay, None, lowest
                 for sub in range(subs):
-                    run_sum, total = value(key + sub * SUB, sub, shift, run_sum, total)
+                    probs = weights(sub, shift)
+                    run_sum = run_sum + jnp.sum(probs, axis=0)
                     if not last:
                         partial = score(half, key + BIG + sub * SUB, at + sub * SUB, sub, partial)
+                    total = value(key + sub * SUB, probs, total)
                 sum_ref[half] = run_sum
                 rescaled(half, total, decay)
                 used_max_ref[half] = shift
@@ -124,12 +126,24 @@
             def _():
                 step(full_steps, True)
 
+            return inner
+
+        def turn_inputs(half):
+            row = geometry(half)[4]
+            qt_ref[half] = q_ref[pl.ds(row, tile), :].T
+            gt_ref[half] = g_ref[pl.ds(row, tile), :].T
+
+        def finish_forward(half):
+            row = geometry(half)[4]
             row_sum = jnp.sum(sum_ref[half], axis=0, keepdims=True)
             out = (ot_ref[half] / row_sum).astype(jnp.bfloat16)
             o_ref[pl.ds(row, tile), :] = out.T
             max_ref[half] = used_max_ref[half] + wide(jnp.log2(row_sum))
             sum_ref[half] = wide(jnp.sum(out.astype(jnp.float32) * gt_ref[half].astype(jnp.float32), axis=0, keepdims=True))
-            return inner
+
+        def finish_backward(half):
+            row = geometry(half)[4]
+            dq_ref[pl.ds(row, tile), :] = (dqt_ref[half] * scale).astype(jnp.bfloat16).T
 
         def grad(half, key, at, size, row):
             log_sum, d_row, total = max_ref[half], sum_ref[half], None
@@ -148,7 +162,6 @@
         def backward_pass(half, inner):
             bound, full_steps, rest_subs, start, row = geometry(half)
             main = start + (rest_subs + 1) * SUB
-            dqt_ref[half] = jnp.zeros((head_dim, tile), jnp.float32)
 
             def step(index, carry):
                 key = pl.multiple_of(index * 2 * BIG, BIG)
@@ -168,12 +181,19 @@
                 def _():
                     grad(half, pl.multiple_of(full_steps * BIG, BIG), pl.multiple_of(start, SUB), (count + 1) * SUB, row)
 
-            dq_ref[pl.ds(row, tile), :] = (dqt_ref[half] * scale).astype(jnp.bfloat16).T
             return inner
 
-        for pass_index, one_pass in enumerate((forward_pass, backward_pass)):
-            between(pair_index, pass_index)
-            lax.fori_loop(0, 2, one_pass, 0)
+        between(pair_index, 0)
+        for half in range(2):
+            turn_inputs(half)
+            dqt_ref[half] = jnp.zeros((head_dim, tile), jnp.float32)
+        lax.fori_loop(0, 2, forward_pass, 0)
+        between(pair_index, 1)
+        for half in range(2):
+            finish_forward(half)
+        lax.fori_loop(0, 2, backward_pass, 0)
+        for half in range(2):
+            finish_backward(half)
         return carry
 
     lax.fori_loop(0, half_len // POS, pair, 0)
@@ -183,7 +203,7 @@
     strip_rows = (seq_len // SUB + 3 + BIG // SUB) * SUB
     return [
         pltpu.VMEM((strip_rows, tile), jnp.float32),
-        pltpu.VMEM((BIG, tile), jnp.float32),
+        pltpu.VMEM((2, BIG, tile), jnp.float32),
         pltpu.VMEM((2, head_dim, tile), jnp.bfloat16),
         pltpu.VMEM((2, head_dim, tile), jnp.bfloat16),
         pltpu.VMEM((2, head_dim, tile), jnp.float32),
@@ -197,7 +217,7 @@
 MESH = pl.DeviceIdType.MESH
 SLOTS = 6
 
-GATHER_AT = {1: (-1, 1, 3, 4, 5), 2: (0, 2, 4, 7, 9), 3: (1, 5, 8, 10, 13), 4: (11, 14, 17, 18, 21)}
+GATHER_AT = {1: (-1, 1, 3, 4, 5), 2: (0, 2, 5, 6, 9), 3: (1, 5, 8, 10, 15), 4: (11, 14, 16, 19, 22)}
 
 
 def _gather_at(seq):
@@ -467,7 +487,8 @@
     reduce_events = {
         (0, 1): reduce_peer_send,
         (1, 1): reduce_begin,
-        (3, 1): steps((2, True), (3, False)),
+        (2, 1): steps((2, True)),
+        (3, 1): steps((3, False)),
         (4, 1): steps((3, True)),
         (5, 1): steps((4, False)),
         (0, 2): steps((4, True)),

time: 322 us -> 315 us (0.978)
  Pallas kernels: 312 us -> 305 us
    pallas_call x1, Pallas kernels: 312 us -> 305 us  [local_attention(): pl.pallas_call(functools.partial(_kernel, ctx_size, heads), out_shape=[ro...]
where the time goes in v4:
time: 315 us
  Pallas kernels  305 us (97%)
  local copies, waits for them, and re-layouts  8.8 us (3%)
    pallas_call x1, Pallas kernels, local_attention(): pl.pallas_call(functools.partial(_kernel, ctx_size, heads), out_shape=[ro...  305 us
    unnamed x10, local copies, waits for them, and re-layouts  8.8 us

profile of v4, /device:TPU:21, one launch (start us, length us, event | category | flops | bytes accessed | tf_op | source)
XLA Modules:
  0.0 314.7 jit_solution(644564330588797254)
XLA Ops:
  0.6 305.2 %shard_map.75 = (bf16[6,3072,128]{2,1,0:T(8,128)(2,1)}, bf16[6,3072,128]{2,1,0:T(8,128)(2,1)}, bf16[6,384,128]{2,1,0:T(8,128)(2,1)}, bf16[6,384,128]{2,1,0:T(8,128)(2,1)}, bf16[6,32,384,128]{3,2,1,0:T(8,128)(2,1)}) custom-call(bf16[6,3072,128]{2,1,0:T(8,128)(2,1)} %bitcast.16, bf16[6,3072,128]{2,1,0:T(8,128)(2,1)} %bitcast.17, ...), custom_call_target="tpu_custom_call" | custom-call | flops 99999997952 | bytes 100000000 | tf_op jit(solution)/shard_map/pallas_call | solution.py:608
  305.9 0.0 copy-start
  305.9 5.0 %copy.14 = bf16[6,384,8,128]{3,2,1,0:T(8,128)(2,1)} copy(bf16[6,384,8,128]{3,2,1,0:T(8,128)(2,1)} %bitcast.13) | data formatting | bytes 9437184
  310.8 0.0 copy-done
  310.8 0.0 copy-start.2
  310.8 0.0 copy-start.1
  310.8 2.2 copy.15
  313.0 0.0 copy-done.2
  313.0 0.8 copy.16
  313.9 0.0 copy-done.1
  313.9 0.8 copy.17
Async XLA Ops:
  305.9 5.0 %copy-start = (bf16[6,3072,128]{2,1,0:T(8,128)(2,1)S(1)}, bf16[6,3072,128]{2,1,0:T(8,128)(2,1)}, u32[]{:S(2)}) copy-start(bf16[6,3072,128]{2,1,0:T(8,128)(2,1)} %get-tuple-element.9) | copy-start | bytes 14155780
  310.8 2.2 copy-start.2
  310.8 3.0 copy-start.1

commit v5 on v4

--- a/solution.py
+++ b/solution.py
@@ -34,6 +34,8 @@
     log2_scale = scale * math.log2(math.e)
     last_piece = 2 * ctx_size - 1
 
+    lowest = jnp.full((8, tile), MASK_VALUE, jnp.float32)
+
     def wide(row):
         return jnp.broadcast_to(row, (8, tile))
 
@@ -75,58 +77,69 @@
         def rescaled(half, total, decay):
             ot_ref[half] = (fold(ot_ref[half]) * decay[None]).reshape(head_dim, tile) + total
 
-        def forward_pass(half, inner):
+        def value_step(half, index, row_scores):
+            key = pl.multiple_of((index - 1) * BIG, BIG)
+            shift = max_ref[half]
+            decay = jnp.exp2(used_max_ref[half] - shift)
+            run_sum, total = sum_ref[half] * decay, None
+            for sub in range(subs):
+                probs = weights(sub, shift)
+                run_sum = run_sum + jnp.sum(probs, axis=0)
+                row_scores(sub)
+                total = value(key + sub * SUB, probs, total)
+            sum_ref[half] = run_sum
+            rescaled(half, total, decay)
+            used_max_ref[half] = shift
+
+        def forward_start(half, behind):
             bound, full_steps, rest_subs, start, row = geometry(half)
-            lowest = jnp.full((8, tile), MASK_VALUE, jnp.float32)
             for count in range(subs):
-
-                @pl.when(rest_subs == count)
-                def _():
-                    key, at = pl.multiple_of(full_steps * BIG, BIG), pl.multiple_of(start, SUB)
-                    partial = lowest
-                    for sub in range(count + 1):
-                        partial = score(half, key + sub * SUB, at + sub * SUB, sub, partial, bound if sub == count else None, 1)
-                    shift, ahead = top(partial), partial
-                    for sub in range(subs):
-                        ahead = score(half, sub * SUB, at + (count + 1 + sub) * SUB, sub, ahead)
-                    run_sum, total = jnp.zeros((8, tile), jnp.float32), None
-                    for sub in range(count + 1):
-                        probs = weights(sub, shift, 1)
-                        run_sum, total = run_sum + jnp.sum(probs, axis=0), value(key + sub * SUB, probs, total)
-                    ot_ref[half] = total
-                    sum_ref[half] = run_sum
-                    used_max_ref[half] = shift
-                    max_ref[half] = jnp.where(full_steps > 0, top(ahead), shift)
-
-            def step(index, last):
-                key = pl.multiple_of((index - 1) * BIG, BIG)
+                for flag in (False, True):
+                    is_behind, has_main = (flag, True) if half else (False, flag)
+
+                    @pl.when((rest_subs == count) & (((behind if half else full_steps) > 0) == flag))
+                    def _():
+                        key, at = pl.multiple_of(full_steps * BIG, BIG), pl.multiple_of(start, SUB)
+                        partial = lowest
+                        for sub in range(count + 1):
+                            last_keys = bound if sub == count else None
+                            partial = score(half, key + sub * SUB, at + sub * SUB, sub, partial, last_keys, 1)
+                        ahead = [partial]
+
+                        def first_block(sub):
+                            ahead[0] = score(half, sub * SUB, at + (count + 1 + sub) * SUB, sub, ahead[0])
+
+                        if is_behind:
+                            value_step(1 - half, behind, first_block)
+                        elif has_main:
+                            for sub in range(subs):
+                                first_block(sub)
+                        shift = top(partial)
+                        run_sum, total = jnp.zeros((8, tile), jnp.float32), None
+                        for sub in range(count + 1):
+                            probs = weights(sub, shift, 1)
+                            run_sum, total = run_sum + jnp.sum(probs, axis=0), value(key + sub * SUB, probs, total)
+                        ot_ref[half] = total
+                        sum_ref[half] = run_sum
+                        used_max_ref[half] = shift
+                        max_ref[half] = top(ahead[0]) if has_main else shift
+
+        def forward_rest(half):
+            _, full_steps, rest_subs, start, _ = geometry(half)
+
+            def step(index, carry):
                 at = pl.multiple_of(start + (rest_subs + 1) * SUB + index * BIG, SUB)
+                partial = [lowest]
+
+                def next_block(sub):
+                    partial[0] = score(half, pl.multiple_of(index * BIG, BIG) + sub * SUB, at + sub * SUB, sub, partial[0])
+
                 shift = max_ref[half]
-                decay = jnp.exp2(used_max_ref[half] - shift)
-                run_sum, total, partial = sum_ref[half] * decay, None, lowest
-                for sub in range(subs):
-                    probs = weights(sub, shift)
-                    run_sum = run_sum + jnp.sum(probs, axis=0)
-                    if not last:
-                        partial = score(half, key + BIG + sub * SUB, at + sub * SUB, sub, partial)
-                    total = value(key + sub * SUB, probs, total)
-                sum_ref[half] = run_sum
-                rescaled(half, total, decay)
-                used_max_ref[half] = shift
-                if not last:
-                    max_ref[half] = jnp.maximum(shift, top(partial))
-
-            def inner_step(index, carry):
-                step(index, False)
+                value_step(half, index, next_block)
+                max_ref[half] = jnp.maximum(shift, top(partial[0]))
                 return carry
 
-            lax.fori_loop(1, full_steps, inner_step, 0)
-
-            @pl.when(full_steps > 0)
-            def _():
-                step(full_steps, True)
-
-            return inner
+            lax.fori_loop(1, full_steps, step, 0)
 
         def turn_inputs(half):
             row = geometry(half)[4]
@@ -187,7 +200,12 @@
         for half in range(2):
             turn_inputs(half)
             dqt_ref[half] = jnp.zeros((head_dim, tile), jnp.float32)
-        lax.fori_loop(0, 2, forward_pass, 0)
+        low_steps, high_steps = geometry(0)[1], geometry(1)[1]
+        forward_start(0, None)
+        forward_rest(0)
+        forward_start(1, low_steps)
+        forward_rest(1)
+        value_step(1, high_steps, lambda sub: None)
         between(pair_index, 1)
         for half in range(2):
             finish_forward(half)
@@ -235,6 +253,7 @@
         part,
         ring_in,
         out_buf,
+        first_recv,
         gather_recv,
         gather_send,
         gather_peer_recv,
@@ -287,32 +306,31 @@
             return [kv_buf.at[0, which, piece_rows(dev, half), :] for half in range(2)]
         return [kv_all.at[seq, 2 * dev + which]]
 
-    def send_shard(sources, seq, dev, which, targets):
-        for target, send_sem, recv_sem in targets:
-            for source, place in zip(sources, shard_refs(seq, dev, which)):
-                remote(source, place, send_sem, recv_sem, target).start()
-
-    def to_side(way, seq, which, hop):
-        return sides[way], gather_send.at[way, seq], gather_recv.at[way, which, seq, hop]
-
-    def to_peer(seq):
-        return peer, gather_peer_send.at[seq], gather_peer_recv.at[seq]
+    def arrived(way, seq, which, hop, part_index):
+        return first_recv.at[way, which, part_index, hop] if seq == 0 else gather_recv.at[way, which, seq, hop]
+
+    def send_part(source, place, seq, which, part_index, hops):
+        remote(source, place, gather_peer_send.at[seq], gather_peer_recv.at[seq], peer).start()
+        for way, hop in hops:
+            remote(source, place, gather_send.at[way, seq], arrived(way, seq, which, hop, part_index), sides[way]).start()
 
     def gather_send_own(seq):
         for which, source in enumerate((k_hbm, v_hbm)):
             sources = [source.at[seq]]
             if seq == 0:
                 sources = [source.at[seq, pl.ds(half * half_len, half_len), :] for half in range(2)]
-            send_shard(sources, seq, me, which, [to_side(0, seq, which, 0), to_side(1, seq, which, 0), to_peer(seq)])
+            for part_index, place in enumerate(shard_refs(seq, me, which)):
+                send_part(sources[part_index], place, seq, which, part_index, [(0, 0), (1, 0)])
 
     def gather_arrival(seq, hop):
         for which in range(2):
-            for way in range(2) if hop < 4 else (which,):
-                origin = device(chip - hop if way == 0 else chip + hop, core)
-                refs = shard_refs(seq, origin, which)
-                wait_recv(kv_all.at[0, 0], gather_recv.at[way, which, seq, hop - 1], sides[way])
-                onward = [to_side(way, seq, which, hop)] if hop < (4 if way == which else 3) else []
-                send_shard(refs, seq, origin, which, onward + [to_peer(seq)])
+            for part_index in range(2 if seq == 0 else 1):
+                for way in range(2) if hop < 4 else (which,):
+                    origin = device(chip - hop if way == 0 else chip + hop, core)
+                    place = shard_refs(seq, origin, which)[part_index]
+                    wait_recv(place, arrived(way, seq, which, hop - 1, part_index), sides[way])
+                    onward = [(way, hop)] if hop < (4 if way == which else 3) else []
+                    send_part(place, place, seq, which, part_index, onward)
 
     def drain(seq, carry):
         for way in range(2):
@@ -624,6 +642,7 @@
                 pltpu.VMEM((2, ctx_size, shard_len, head_dim), jnp.float32),
                 pltpu.VMEM((2, 2, 2, 4, shard_len, head_dim), jnp.float32),
                 pltpu.VMEM((2, 2, shard_len, head_dim), jnp.bfloat16),
+                dma((2, 2, 2, 4)),
                 dma((2, 2, batch, 4)),
                 dma((2, batch)),
                 dma((batch,)),

time: 315 us -> 312 us (level)
  no operation moved by 1% of the time
where the time goes in v5:
time: 312 us
  Pallas kernels  303 us (97%)
  local copies, waits for them, and re-layouts  8.8 us (3%)
    pallas_call x1, Pallas kernels, local_attention(): pl.pallas_call(functools.partial(_kernel, ctx_size, heads), out_shape=[ro...  303 us
    unnamed x10, local copies, waits for them, and re-layouts  8.8 us

profile of v5, /device:TPU:21, one launch (start us, length us, event | category | flops | bytes accessed | tf_op | source)
XLA Modules:
  0.0 312.2 jit_solution(3568120498951595987)
XLA Ops:
  0.6 302.7 %shard_map.75 = (bf16[6,3072,128]{2,1,0:T(8,128)(2,1)}, bf16[6,3072,128]{2,1,0:T(8,128)(2,1)}, bf16[6,384,128]{2,1,0:T(8,128)(2,1)}, bf16[6,384,128]{2,1,0:T(8,128)(2,1)}, bf16[6,32,384,128]{3,2,1,0:T(8,128)(2,1)}) custom-call(bf16[6,3072,128]{2,1,0:T(8,128)(2,1)} %bitcast.16, bf16[6,3072,128]{2,1,0:T(8,128)(2,1)} %bitcast.17, ...), custom_call_target="tpu_custom_call" | custom-call | flops 99999997952 | bytes 100000000 | tf_op jit(solution)/shard_map/pallas_call | solution.py:626
  303.4 0.0 copy-start
  303.4 5.0 %copy.14 = bf16[6,384,8,128]{3,2,1,0:T(8,128)(2,1)} copy(bf16[6,384,8,128]{3,2,1,0:T(8,128)(2,1)} %bitcast.13) | data formatting | bytes 9437184
  308.4 0.0 copy-done
  308.4 0.0 copy-start.2
  308.4 0.0 copy-start.1
  308.4 2.2 copy.15
  310.5 0.0 copy-done.2
  310.6 0.8 copy.16
  311.4 0.0 copy-done.1
  311.4 0.8 copy.17
Async XLA Ops:
  303.4 5.0 %copy-start = (bf16[6,3072,128]{2,1,0:T(8,128)(2,1)S(1)}, bf16[6,3072,128]{2,1,0:T(8,128)(2,1)}, u32[]{:S(2)}) copy-start(bf16[6,3072,128]{2,1,0:T(8,128)(2,1)} %get-tuple-element.9) | copy-start | bytes 14155780
  308.4 2.2 copy-start.2
  308.4 3.0 copy-start.1
